TPU v7x, 32 devices: a whole 2x2x4 slice. The times are simulated.
32 devices in a mesh: dp: 16 (over z, x, core), tensor: 2 (over y).
Axes of the slice: x: 2, y: 2, z: 4, core: 2. Of those that a mesh axis runs over, the one named last changes fastest.
Arguments:
- tokens: bfloat16 [32768, 640], P(('dp', 'tensor')), may hold values from -6 to 6
- window_offsets: int32 [32], P('dp'), may hold values from 0 to 2047, as said below
- lengths: int32 [32], P('dp'), may hold values from 1 to 1024, as said below
- key_mask: int32 [32, 1024], P('dp'), may hold values from 0 to 1, as said below
- ln1_gain: float32 [640], replicated, may hold values from 0.5 to 1.5
- ln1_bias: float32 [640], replicated, may hold values from -1.5 to 1.5
- w_qkv: bfloat16 [3, 640, 640], P(None, None, 'tensor'), may hold values from -0.3125 to 0.3125
- qv_bias: float32 [2, 640], P(None, 'tensor'), may hold values from -1.5 to 1.5
- w_out: bfloat16 [640, 640], P('tensor'), may hold values from -1 to 1
- out_bias: float32 [640], replicated, may hold values from -1.5 to 1.5
- ln2_gain: float32 [640], replicated, may hold values from 0.5 to 1.5
- ln2_bias: float32 [640], replicated, may hold values from -1.5 to 1.5
- w_up: bfloat16 [640, 5120], P(None, 'tensor'), may hold values from -0.25 to 0.25
- up_bias: float32 [5120], P('tensor'), may hold values from -2.5 to 2.5
- w_down: bfloat16 [5120, 640], P('tensor'), may hold values from -0.15625 to 0.15625
- down_bias: float32 [640], replicated, may hold values from -1.5 to 1.5
- out_grad: bfloat16 [32768, 640], P(('dp', 'tensor')), may hold values from -6 to 6
Outputs:
- layer_out: bfloat16 [32768, 640], P(('dp', 'tensor'))
- tokens_grad: bfloat16 [32768, 640], P(('dp', 'tensor'))
- grad_ln1_gain: float32 [640], replicated
- grad_ln1_bias: float32 [640], replicated
- grad_w_qkv: float32 [3, 640, 640], P(None, None, 'tensor')
- grad_qv_bias: float32 [2, 640], P(None, 'tensor')
- grad_w_out: float32 [640, 640], P('tensor')
- grad_out_bias: float32 [640], replicated
- grad_ln2_gain: float32 [640], replicated
- grad_ln2_bias: float32 [640], replicated
- grad_w_up: float32 [640, 5120], P(None, 'tensor')
- grad_up_bias: float32 [5120], P('tensor')
- grad_w_down: float32 [5120, 640], P('tensor')
- grad_down_bias: float32 [640], replicated
Inputs may be any that keep to these rules, and one draw needn't show every extreme that they name: `window_offsets`: rows 2i and 2i+1 form pair i. Either both offsets are 0, or the second exceeds the first by 512 to 1024. Rows 0 and 1 are of the second kind, with offsets 1024 - 1 and 2047; rows 2 and 3 are of the first kind. `lengths`: both rows of a pair whose second offset exceeds its first have length 1024. key_mask[r, 0] is 1 for every row r.
All inputs are finite; a program needn't handle non-finite values.
Results may differ from a plain program's by a relative error of at most 0.014.
The roundings to bfloat16 on the way count: a program that leaves them out, or rounds other values in their place, can miss the bound.
Values may be sent and summed in bfloat16 or wider, within the bound.
A program may use at most 320 MiB of HBM per device.

v0:
```python
import math

import jax
import jax.numpy as jnp
from jax import lax
from jax.sharding import PartitionSpec as P

HEAD = 32


epsilon = 1e-05
masked_score = -1000000000.0


def layer_norm(inputs, gain_vec, bias_vec):
    center = inputs - jnp.mean(inputs, axis=-1, keepdims=True)
    spread = jnp.mean(center * center, axis=-1, keepdims=True)
    return center * lax.rsqrt(spread + epsilon) * gain_vec + bias_vec


def gelu_exact(inputs):
    return jax.nn.gelu(inputs, approximate=False)


def pair_keys(offsets, item_lengths, key_flags):
    seq_len = key_flags.shape[1]
    column = lax.broadcasted_iota(jnp.int32, (2, seq_len), 1)
    second = lax.broadcasted_iota(jnp.int32, (2, seq_len), 0) == 1
    joined = offsets[1] > offsets[0]
    repeat = second & joined & (offsets[1] + column < offsets[0] + seq_len)
    live_keys = (key_flags == 1) & (column < item_lengths[:, None]) & jnp.logical_not(repeat)
    return (live_keys.reshape(2 * seq_len), joined)


def allowed_block(live_keys, joined, first_row, row_count, seq_len):
    query_row = (first_row + lax.iota(jnp.int32, row_count)) // seq_len
    key_row = lax.iota(jnp.int32, 2 * seq_len) // seq_len
    return live_keys[None, :] & (joined | (query_row[:, None] == key_row[None, :]))


def block_scores(query_part, key_pair, live_keys, joined, block_index, block_rows, score_scale):
    pair_span = key_pair.shape[0]
    scores = (
        jnp.einsum("qhe,khe->hqk", query_part, key_pair, preferred_element_type=jnp.float32)
        * score_scale
    )
    allowed = allowed_block(live_keys, joined, block_index * block_rows, block_rows, pair_span // 2)
    return jnp.where(allowed[None], scores, masked_score)


def attention_forward(query_pair, key_pair, value_pair, live_keys, joined, block_rows):
    pair_span, heads_here, head_size = query_pair.shape
    score_scale = 1.0 / math.sqrt(head_size)
    blocks = pair_span // block_rows
    query_blocks = query_pair.reshape(blocks, block_rows, heads_here, head_size)

    def one_block(block_items):
        block_index, query_part = block_items
        scores = block_scores(
            query_part, key_pair, live_keys, joined, block_index, block_rows, score_scale
        )
        row_max = jnp.max(scores, axis=-1, keepdims=True)
        exponent = jnp.exp(scores - row_max)
        row_total = jnp.sum(exponent, axis=-1, keepdims=True)
        prob_low = (exponent / row_total).astype(jnp.bfloat16)
        mixed_heads = jnp.einsum(
            "hqk,khe->qhe", prob_low, value_pair, preferred_element_type=jnp.float32
        )
        return (mixed_heads, (row_max + jnp.log(row_total))[..., 0])

    mixed_heads, log_norm = lax.map(one_block, (jnp.arange(blocks, dtype=jnp.int32), query_blocks))
    return (mixed_heads.reshape(pair_span, heads_here * head_size).astype(jnp.bfloat16), log_norm)


def attention_backward(
    query_pair, key_pair, value_pair, grad_pair, log_norm, live_keys, joined, block_rows
):
    pair_span, heads_here, head_size = query_pair.shape
    score_scale = 1.0 / math.sqrt(head_size)
    blocks = pair_span // block_rows
    query_blocks = query_pair.reshape(blocks, block_rows, heads_here, head_size)
    grad_blocks = grad_pair.reshape(blocks, block_rows, heads_here, head_size)

    def one_block(carry_in, block_items):
        grad_keys, grad_values = carry_in
        block_index, query_part, grad_part, norm_part = block_items
        scores = block_scores(
            query_part, key_pair, live_keys, joined, block_index, block_rows, score_scale
        )
        probs = jnp.exp(scores - norm_part[..., None])
        grad_probs = jnp.einsum(
            "qhe,khe->hqk", grad_part, value_pair, preferred_element_type=jnp.float32
        )
        inner_sum = jnp.sum(probs * grad_probs, axis=-1, keepdims=True)
        grad_scores = (probs * (grad_probs - inner_sum)).astype(jnp.bfloat16)
        grad_query = (
            jnp.einsum("hqk,khe->qhe", grad_scores, key_pair, preferred_element_type=jnp.float32)
            * score_scale
        )
        grad_keys = (
            grad_keys
            + jnp.einsum(
                "hqk,qhe->khe", grad_scores, query_part, preferred_element_type=jnp.float32
            )
            * score_scale
        )
        grad_values = grad_values + jnp.einsum(
            "hqk,qhe->khe",
            probs.astype(jnp.bfloat16),
            grad_part,
            preferred_element_type=jnp.float32,
        )
        return ((grad_keys, grad_values), grad_query)

    zeros_init = jnp.zeros((pair_span, heads_here, head_size), jnp.float32)
    (grad_keys, grad_values), grad_query = lax.scan(
        one_block,
        (zeros_init, zeros_init),
        (jnp.arange(blocks, dtype=jnp.int32), query_blocks, grad_blocks, log_norm),
    )
    flat_shape = (pair_span, heads_here * head_size)
    return (
        grad_query.reshape(flat_shape).astype(jnp.bfloat16),
        grad_keys.reshape(flat_shape).astype(jnp.bfloat16),
        grad_values.reshape(flat_shape).astype(jnp.bfloat16),
    )


def body(
    tokens,
    window_offsets,
    lengths,
    key_mask,
    ln1_gain,
    ln1_bias,
    w_qkv,
    qv_bias,
    w_out,
    out_bias,
    ln2_gain,
    ln2_bias,
    w_up,
    up_bias,
    w_down,
    down_bias,
    out_grad,
):
    seq_len = key_mask.shape[1]
    pair_count = window_offsets.shape[0] // 2
    pair_span = 2 * seq_len
    local_width = w_qkv.shape[2]
    heads_here = local_width // HEAD
    block_rows = math.gcd(512, pair_span)
    shaped = (pair_count, pair_span, heads_here, HEAD)
    tokens_f = tokens.astype(jnp.float32)
    normed = layer_norm(tokens_f, ln1_gain, ln1_bias).astype(jnp.bfloat16)
    normed_all = lax.all_gather(normed, "tensor", axis=0, tiled=True)
    projected = jnp.einsum("td,cde->tce", normed_all, w_qkv, preferred_element_type=jnp.float32)
    query_tok = (projected[:, 0] + qv_bias[0]).astype(jnp.bfloat16).reshape(shaped)
    key_tok = projected[:, 1].astype(jnp.bfloat16).reshape(shaped)
    value_tok = (projected[:, 2] + qv_bias[1]).astype(jnp.bfloat16).reshape(shaped)
    pair_index = 0
    live_keys, joined = pair_keys(window_offsets, lengths, key_mask)
    pair_masks = [(live_keys, joined)]
    mixed_heads, log_norm = attention_forward(
        query_tok[pair_index],
        key_tok[pair_index],
        value_tok[pair_index],
        live_keys,
        joined,
        block_rows,
    )
    norms_list = [log_norm]
    rows_part = mixed_heads
    attn_out = (
        lax.psum_scatter(
            jnp.dot(rows_part, w_out, preferred_element_type=jnp.float32),
            "tensor",
            scatter_dimension=0,
            tiled=True,
        )
        + out_bias
    )
    residual_mid = tokens_f + attn_out
    normed_mid = layer_norm(residual_mid, ln2_gain, ln2_bias).astype(jnp.bfloat16)
    normed_mid_all = lax.all_gather(normed_mid, "tensor", axis=0, tiled=True)
    upper = jnp.dot(normed_mid_all, w_up, preferred_element_type=jnp.float32) + up_bias
    activated = gelu_exact(upper).astype(jnp.bfloat16)
    rows_part = activated
    branch = (
        lax.psum_scatter(
            jnp.dot(rows_part, w_down, preferred_element_type=jnp.float32).astype(jnp.bfloat16),
            "tensor",
            scatter_dimension=0,
            tiled=True,
        ).astype(jnp.float32)
        + down_bias
    )
    layer_out = (residual_mid + branch).astype(jnp.bfloat16)
    grad_all = lax.all_gather(out_grad, "tensor", axis=0, tiled=True)
    grad_w_down = jnp.einsum("tf,td->fd", activated, grad_all, preferred_element_type=jnp.float32)
    grad_act = jnp.einsum("td,fd->tf", grad_all, w_down, preferred_element_type=jnp.float32)
    _, gelu_back = jax.vjp(gelu_exact, upper)
    grad_upper = gelu_back(grad_act)[0].astype(jnp.bfloat16)
    grad_w_up = jnp.einsum(
        "td,tf->df", normed_mid_all, grad_upper, preferred_element_type=jnp.float32
    )
    grad_up_bias = jnp.sum(grad_upper, axis=0, dtype=jnp.float32)
    rows_part = grad_upper
    grad_normed_mid = lax.psum_scatter(
        jnp.einsum("tf,df->td", rows_part, w_up, preferred_element_type=jnp.float32),
        "tensor",
        scatter_dimension=0,
        tiled=True,
    )
    _, norm2_back = jax.vjp(layer_norm, residual_mid, ln2_gain, ln2_bias)
    grad_mid_part, grad_ln2_gain, grad_ln2_bias = norm2_back(grad_normed_mid)
    grad_mid = out_grad.astype(jnp.float32) + grad_mid_part
    grad_mid_low = grad_mid.astype(jnp.bfloat16)
    grad_mid_all = lax.all_gather(grad_mid_low, "tensor", axis=0, tiled=True)
    grad_w_out = jnp.einsum(
        "te,td->ed", mixed_heads, grad_mid_all, preferred_element_type=jnp.float32
    )
    grad_heads = jnp.einsum(
        "td,ed->te", grad_mid_all, w_out, preferred_element_type=jnp.float32
    ).astype(jnp.bfloat16)
    grad_heads = grad_heads.reshape(shaped)
    pair_index = 0
    live_keys, joined = pair_masks[pair_index]
    grad_query, grad_key, grad_value = attention_backward(
        query_tok[pair_index],
        key_tok[pair_index],
        value_tok[pair_index],
        grad_heads[pair_index],
        norms_list[pair_index],
        live_keys,
        joined,
        block_rows,
    )
    grad_qkv = jnp.stack([grad_query, grad_key, grad_value], axis=1)
    grad_w_qkv = jnp.einsum("td,tce->cde", normed_all, grad_qkv, preferred_element_type=jnp.float32)
    grad_qv_bias = jnp.stack(
        [
            jnp.sum(grad_query, axis=0, dtype=jnp.float32),
            jnp.sum(grad_value, axis=0, dtype=jnp.float32),
        ]
    )
    rows_part = grad_qkv
    grad_normed = lax.psum_scatter(
        jnp.einsum("tce,cde->td", rows_part, w_qkv, preferred_element_type=jnp.float32),
        "tensor",
        scatter_dimension=0,
        tiled=True,
    )
    _, norm1_back = jax.vjp(layer_norm, tokens_f, ln1_gain, ln1_bias)
    grad_tok_part, grad_ln1_gain, grad_ln1_bias = norm1_back(grad_normed)
    tokens_grad = (grad_mid + grad_tok_part).astype(jnp.bfloat16)
    grad_out_bias = jnp.sum(grad_mid_low, axis=0, dtype=jnp.float32)
    grad_down_bias = jnp.sum(out_grad, axis=0, dtype=jnp.float32)
    grad_ln1_gain, grad_ln1_bias, grad_ln2_gain, grad_ln2_bias, grad_out_bias, grad_down_bias = (
        lax.psum(
            (
                grad_ln1_gain,
                grad_ln1_bias,
                grad_ln2_gain,
                grad_ln2_bias,
                grad_out_bias,
                grad_down_bias,
            ),
            ("dp", "tensor"),
        )
    )
    grad_w_qkv, grad_qv_bias, grad_w_out, grad_w_up, grad_up_bias, grad_w_down = lax.psum(
        (grad_w_qkv, grad_qv_bias, grad_w_out, grad_w_up, grad_up_bias, grad_w_down), "dp"
    )
    return (
        layer_out,
        tokens_grad,
        grad_ln1_gain,
        grad_ln1_bias,
        grad_w_qkv,
        grad_qv_bias,
        grad_w_out,
        grad_out_bias,
        grad_ln2_gain,
        grad_ln2_bias,
        grad_w_up,
        grad_up_bias,
        grad_w_down,
        grad_down_bias,
    )


def solution(mesh):
    in_specs = (
        P(("dp", "tensor"), None),
        P("dp"),
        P("dp"),
        P("dp", None),
        P(),
        P(),
        P(None, None, "tensor"),
        P(None, "tensor"),
        P("tensor", None),
        P(),
        P(),
        P(),
        P(None, "tensor"),
        P("tensor"),
        P("tensor", None),
        P(),
        P(("dp", "tensor"), None),
    )
    out_specs = (
        P(("dp", "tensor"), None),
        P(("dp", "tensor"), None),
        P(),
        P(),
        P(None, None, "tensor"),
        P(None, "tensor"),
        P("tensor", None),
        P(),
        P(),
        P(),
        P(None, "tensor"),
        P("tensor"),
        P("tensor", None),
        P(),
    )
    return jax.shard_map(body, mesh=mesh, in_specs=in_specs, out_specs=out_specs, check_vma=False)
```

profile of v0, /device:TPU:0, one launch (start us, length us, event | category | flops | bytes accessed | tf_op | source)
XLA Modules:
  0.0 1586.4 jit_solution(10227022406443047628)
XLA Ops:
  17.3 38.3 %all-gather.5.cloned.1.call-done = bf16[2048,640]{1,0:T(8,128)(2,1)} async-done(((bf16[1024,640]{1,0:T(8,128)(2,1)}), bf16[2048,640]{1,0:T(8,128)(2,1)}) %all-gather.5.cloned.1.call-update) | async-done | bytes 2621456 | tf_op jit(solution)/shard_map/all_gather | solution.py:157
  76.3 232.8 %while.35 = (s32[]{:T(128)}, bf16[4,512,10,32]{1,3,2,0:T(8,128)(2,1)}, f32[4,10,512]{2,1,0:T(8,128)}, pred[2,1024]{1,0:T(4,128)(4,1)}, pred[]{:T(512)}, /*index=...) while((s32[]{:T(128)}, ...), condition=%wide.wide.region_5.6_spmd, body=%wide.wide.region_2.5_spmd.sunk | while | flops 1471171584 | bytes 149580016 | solution.py:71
  78.5 18.6 %fusion.158 = (f32[10,512]{1,0:T(8,128)S(1)}, f32[10,512,2048]{2,1,0:T(8,128)}) fusion(pred[512,2048]{1,0:T(8,128)(4,1)S(1)} %or_and_fusion.6, bf16[2048,10,32]{0,2,1:T(8,128)(2,1)} %get-tuple-element.761, bf16[4,512,10,32]{1,3,2,0:T(8,128)(2,1)} %get-tuple-element.760, s32[]{:T(128)S(6)} %copy.48), kind=kOutput, calls=%fused_computation.3.clone.clone.1 | convolution fusion | flops 702540800 | bytes 44650500 | tf_op jit(solution)/shard_map/while/body/eval_jaxpr/qhe,khe->hqk/dot_general | solution.py:44
  97.0 19.3 %fusion.159 = f32[10,512]{1,0:T(8,128)S(1)} fusion(f32[10,512,2048]{2,1,0:T(8,128)} %get-tuple-element.713, f32[10,512]{1,0:T(8,128)S(1)} %get-tuple-element.714, pred[512,2048]{1,0:T(8,128)(4,1)S(1)} %or_and_fusion.6), kind=kLoop, calls=%fused_computation.4.clone.clone.1 | loop fusion | flops 41937920 | bytes 43032576 | tf_op jit(solution)/shard_map/while/body/eval_jaxpr/reduce_sum | solution.py:64
  116.4 16.9 %fusion.160 = bf16[4,512,10,32]{1,3,2,0:T(8,128)(2,1)S(1)} fusion(bf16[4,512,10,32]{1,3,2,0:T(8,128)(2,1)S(1)} %copy-done.22, s32[]{:T(128)S(6)} %copy.48, bf16[2048,10,32]{0,2,1:T(8,128)(2,1)S(1)} %copy-done.9, f32[10,512,2048]{2,1,0:T(8,128)} %get-tuple-element.713, f32[10,512]{1,0:T(8,128)S(1)} %fusion.159, ...), kind=kOutput, calls=%fused_computation.8.clone.clone.1 | convolution fusion | flops 723517440 | bytes 45023236 | tf_op jit(solution)/shard_map/while/body/eval_jaxpr/hqk,khe->qhe/dot_general | solution.py:66
  136.5 18.6 %fusion.158 = (f32[10,512]{1,0:T(8,128)S(1)}, f32[10,512,2048]{2,1,0:T(8,128)}) fusion(pred[512,2048]{1,0:T(8,128)(4,1)S(1)} %or_and_fusion.6, bf16[2048,10,32]{0,2,1:T(8,128)(2,1)} %get-tuple-element.761, bf16[4,512,10,32]{1,3,2,0:T(8,128)(2,1)} %get-tuple-element.760, s32[]{:T(128)S(6)} %copy.48), kind=kOutput, calls=%fused_computation.3.clone.clone.1 | convolution fusion | flops 702540800 | bytes 44650500 | tf_op jit(solution)/shard_map/while/body/eval_jaxpr/qhe,khe->hqk/dot_general | solution.py:44
  155.1 19.3 %fusion.159 = f32[10,512]{1,0:T(8,128)S(1)} fusion(f32[10,512,2048]{2,1,0:T(8,128)} %get-tuple-element.713, f32[10,512]{1,0:T(8,128)S(1)} %get-tuple-element.714, pred[512,2048]{1,0:T(8,128)(4,1)S(1)} %or_and_fusion.6), kind=kLoop, calls=%fused_computation.4.clone.clone.1 | loop fusion | flops 41937920 | bytes 43032576 | tf_op jit(solution)/shard_map/while/body/eval_jaxpr/reduce_sum | solution.py:64
  174.5 16.9 %fusion.160 = bf16[4,512,10,32]{1,3,2,0:T(8,128)(2,1)S(1)} fusion(bf16[4,512,10,32]{1,3,2,0:T(8,128)(2,1)S(1)} %copy-done.22, s32[]{:T(128)S(6)} %copy.48, bf16[2048,10,32]{0,2,1:T(8,128)(2,1)S(1)} %copy-done.9, f32[10,512,2048]{2,1,0:T(8,128)} %get-tuple-element.713, f32[10,512]{1,0:T(8,128)S(1)} %fusion.159, ...), kind=kOutput, calls=%fused_computation.8.clone.clone.1 | convolution fusion | flops 723517440 | bytes 45023236 | tf_op jit(solution)/shard_map/while/body/eval_jaxpr/hqk,khe->qhe/dot_general | solution.py:66
  194.6 18.6 %fusion.158 = (f32[10,512]{1,0:T(8,128)S(1)}, f32[10,512,2048]{2,1,0:T(8,128)}) fusion(pred[512,2048]{1,0:T(8,128)(4,1)S(1)} %or_and_fusion.6, bf16[2048,10,32]{0,2,1:T(8,128)(2,1)} %get-tuple-element.761, bf16[4,512,10,32]{1,3,2,0:T(8,128)(2,1)} %get-tuple-element.760, s32[]{:T(128)S(6)} %copy.48), kind=kOutput, calls=%fused_computation.3.clone.clone.1 | convolution fusion | flops 702540800 | bytes 44650500 | tf_op jit(solution)/shard_map/while/body/eval_jaxpr/qhe,khe->hqk/dot_general | solution.py:44
  213.2 19.3 %fusion.159 = f32[10,512]{1,0:T(8,128)S(1)} fusion(f32[10,512,2048]{2,1,0:T(8,128)} %get-tuple-element.713, f32[10,512]{1,0:T(8,128)S(1)} %get-tuple-element.714, pred[512,2048]{1,0:T(8,128)(4,1)S(1)} %or_and_fusion.6), kind=kLoop, calls=%fused_computation.4.clone.clone.1 | loop fusion | flops 41937920 | bytes 43032576 | tf_op jit(solution)/shard_map/while/body/eval_jaxpr/reduce_sum | solution.py:64
  232.5 16.9 %fusion.160 = bf16[4,512,10,32]{1,3,2,0:T(8,128)(2,1)S(1)} fusion(bf16[4,512,10,32]{1,3,2,0:T(8,128)(2,1)S(1)} %copy-done.22, s32[]{:T(128)S(6)} %copy.48, bf16[2048,10,32]{0,2,1:T(8,128)(2,1)S(1)} %copy-done.9, f32[10,512,2048]{2,1,0:T(8,128)} %get-tuple-element.713, f32[10,512]{1,0:T(8,128)S(1)} %fusion.159, ...), kind=kOutput, calls=%fused_computation.8.clone.clone.1 | convolution fusion | flops 723517440 | bytes 45023236 | tf_op jit(solution)/shard_map/while/body/eval_jaxpr/hqk,khe->qhe/dot_general | solution.py:66
  252.7 18.6 %fusion.158 = (f32[10,512]{1,0:T(8,128)S(1)}, f32[10,512,2048]{2,1,0:T(8,128)}) fusion(pred[512,2048]{1,0:T(8,128)(4,1)S(1)} %or_and_fusion.6, bf16[2048,10,32]{0,2,1:T(8,128)(2,1)} %get-tuple-element.761, bf16[4,512,10,32]{1,3,2,0:T(8,128)(2,1)} %get-tuple-element.760, s32[]{:T(128)S(6)} %copy.48), kind=kOutput, calls=%fused_computation.3.clone.clone.1 | convolution fusion | flops 702540800 | bytes 44650500 | tf_op jit(solution)/shard_map/while/body/eval_jaxpr/qhe,khe->hqk/dot_general | solution.py:44
  271.3 19.3 %fusion.159 = f32[10,512]{1,0:T(8,128)S(1)} fusion(f32[10,512,2048]{2,1,0:T(8,128)} %get-tuple-element.713, f32[10,512]{1,0:T(8,128)S(1)} %get-tuple-element.714, pred[512,2048]{1,0:T(8,128)(4,1)S(1)} %or_and_fusion.6), kind=kLoop, calls=%fused_computation.4.clone.clone.1 | loop fusion | flops 41937920 | bytes 43032576 | tf_op jit(solution)/shard_map/while/body/eval_jaxpr/reduce_sum | solution.py:64
  290.6 16.9 %fusion.160 = bf16[4,512,10,32]{1,3,2,0:T(8,128)(2,1)S(1)} fusion(bf16[4,512,10,32]{1,3,2,0:T(8,128)(2,1)S(1)} %copy-done.22, s32[]{:T(128)S(6)} %copy.48, bf16[2048,10,32]{0,2,1:T(8,128)(2,1)S(1)} %copy-done.9, f32[10,512,2048]{2,1,0:T(8,128)} %get-tuple-element.713, f32[10,512]{1,0:T(8,128)S(1)} %fusion.159, ...), kind=kOutput, calls=%fused_computation.8.clone.clone.1 | convolution fusion | flops 723517440 | bytes 45023236 | tf_op jit(solution)/shard_map/while/body/eval_jaxpr/hqk,khe->qhe/dot_general | solution.py:66
  317.2 65.9 %reduce-scatter.5.cloned.1.call-done = f32[1024,640]{1,0:T(8,128)} async-done(((f32[2048,640]{1,0:T(8,128)}), f32[1024,640]{1,0:T(8,128)}) %reduce-scatter.5.cloned.1.call-update) | async-done | bytes 2621456 | tf_op jit(solution)/shard_map/reduce_scatter | solution.py:176
  389.8 38.5 %all-gather.7.cloned.1.call-done = bf16[2048,640]{1,0:T(8,128)(2,1)} async-done(((bf16[1024,640]{1,0:T(8,128)(2,1)}), bf16[2048,640]{1,0:T(8,128)(2,1)}) %all-gather.7.cloned.1.call-update) | async-done | bytes 2621456 | tf_op jit(solution)/shard_map/all_gather | solution.py:186
  428.4 53.9 %multiply_convert_fusion.1 = (bf16[2048,2560]{1,0:T(8,128)(2,1)}, f32[2048,2560]{1,0:T(8,128)}, f32[2048,2560]{1,0:T(8,128)}) fusion(f32[2560]{0:T(1024)S(1)} %copy-done.68, bf16[2048,640]{1,0:T(8,128)(2,1)} %all-gather.7.cloned.1.call-done, bf16[640,2560]{1,0:T(8,128)(2,1)S(1)} %copy-done), kind=kOutput, calls=%fused_computation.84 | convolution fusion | flops 7056916480 | bytes 58337280 | tf_op jit(solution)/shard_map/dot_general | solution.py:187
  482.2 26.2 %convert_reduce_fusion = (f32[2560]{0:T(1024)}, bf16[2048,2560]{1,0:T(8,128)(2,1)}) fusion(f32[2048,2560]{1,0:T(8,128)} %get-tuple-element.477, bf16[2048,640]{1,0:T(8,128)(2,1)} %all-gather.9.cloned.1.call-done, bf16[2560,640]{1,0:T(8,128)(2,1)} %param.35, f32[2048,2560]{1,0:T(8,128)} %get-tuple-element.491, f32[2560]{0:T(1024)S(1)} %copy-done.68), kind=kOutput, calls=%fused_computation.82 | convolution fusion | flops 6800012800 | bytes 58347520 | tf_op jit(solution)/shard_map/td,fd->tf/dot_general | solution.py:202
  508.4 12.5 fusion.91
  521.0 13.2 convolution_convert_fusion
  534.3 52.5 %reduce-scatter.9.cloned.1.call-done = f32[1024,640]{1,0:T(8,128)} async-done(((f32[2048,640]{1,0:T(8,128)}), f32[1024,640]{1,0:T(8,128)}) %reduce-scatter.9.cloned.1.call-update) | async-done | bytes 2621456 | tf_op jit(solution)/shard_map/reduce_scatter | solution.py:210
  590.1 36.5 %reduce-scatter.7.cloned.1.call-done = bf16[1024,640]{1,0:T(8,128)(2,1)} async-done(((bf16[2048,640]{1,0:T(8,128)(2,1)}), bf16[1024,640]{1,0:T(8,128)(2,1)}) %reduce-scatter.7.cloned.1.call-update) | async-done | bytes 1310736 | tf_op jit(solution)/shard_map/reduce_scatter | solution.py:191
  632.8 39.1 %all-gather.11.cloned.1.call-done = bf16[2048,640]{1,0:T(8,128)(2,1)} async-done(((bf16[1024,640]{1,0:T(8,128)(2,1)}), bf16[2048,640]{1,0:T(8,128)(2,1)}) %all-gather.11.cloned.1.call-update) | async-done | bytes 2621456 | tf_op jit(solution)/shard_map/all_gather | solution.py:220
  678.5 508.3 %while.36 = (s32[]{:T(128)}, f32[2048,10,32]{0,2,1:T(8,128)}, f32[2048,10,32]{0,2,1:T(8,128)}, bf16[4,512,10,32]{1,3,2,0:T(8,128)(2,1)}, bf16[4,512,10,32]{1,3,2...) while((s32[]{:T(128)}, f32[2048,10,32]{0,2,1:T(8,128)}, ...), condition=%wide.wide.region_15.16_spmd.clone, body=%wide.wide.region_13.15_spmd.clone.sunk | while | flops 3519335424 | bytes 366774624 | solution.py:116
  681.8 17.4 %fusion.170 = f32[10,512,2048]{2,1,0:T(8,128)} fusion(bf16[2048,10,32]{0,2,1:T(8,128)(2,1)S(1)} %get-tuple-element.806, bf16[4,512,10,32]{1,3,2,0:T(8,128)(2,1)} %get-tuple-element.802, s32[]{:T(128)S(6)} %copy.58), kind=kOutput, calls=%fused_computation.51.clone.clone.1 | convolution fusion | flops 671088640 | bytes 43581444 | tf_op jit(solution)/shard_map/while/body/eval_jaxpr/qhe,khe->hqk/dot_general | solution.py:44
  699.2 20.0 %select_add_fusion.3 = f32[2048,10,32]{0,2,1:T(8,128)} fusion(f32[2048,10,32]{0,2,1:T(8,128)} %get-tuple-element.784, f32[10,512,2048]{2,1,0:T(8,128)} %fusion.170, f32[10,512]{1,0:T(8,128)S(1)} %dynamic-slice_bitcast_fusion.3, pred[512,2048]{1,0:T(8,128)(4,1)S(1)} %or_and_fusion.7, pred[]{:T(512)S(6)} %compare.36, ...), kind=kOutput, calls=%fused_computation.43.clone.clone.1 | convolution fusion | flops 714342400 | bytes 48582660 | tf_op jit(solution)/shard_map/while/body/eval_jaxpr/hqk,qhe->khe/dot_general | solution.py:107
  719.1 30.2 %multiply_reduce_fusion.6 = (f32[10,512]{1,0:T(8,128)S(1)}, f32[10,512,2048]{2,1,0:T(8,128)}) fusion(f32[10,512,2048]{2,1,0:T(8,128)} %fusion.170, f32[10,512]{1,0:T(8,128)S(1)} %dynamic-slice_bitcast_fusion.3, pred[512,2048]{1,0:T(8,128)(4,1)S(1)} %or_and_fusion.7, bf16[2048,10,32]{0,2,1:T(8,128)(2,1)} %get-tuple-element.809, ...), kind=kOutput, calls=%fused_computation.33.clone.clone.1 | convolution fusion | flops 723512320 | bytes 86614016 | tf_op jit(solution)/shard_map/while/body/eval_jaxpr/qhe,khe->hqk/dot_general | solution.py:91
  749.3 34.2 %multiply_convert_fusion.4 = bf16[10,512,2048]{2,1,0:T(8,128)(2,1)} fusion(f32[10,512,2048]{2,1,0:T(8,128)} %get-tuple-element.728, f32[10,512,2048]{2,1,0:T(8,128)} %fusion.170, f32[10,512]{1,0:T(8,128)S(1)} %get-tuple-element.729, f32[10,512]{1,0:T(8,128)S(1)} %dynamic-slice_bitcast_fusion.3, pred[512,2048]{1,0:T(8,128)(4,1)S(1)} %or_and_fusion.7), kind=kLoop, calls=%fused_computation.32.clone.clone.1 | loop fusion | flops 62914560 | bytes 105947136 | tf_op jit(solution)/shard_map/while/body/eval_jaxpr/convert_element_type | solution.py:95
  783.5 10.7 fusion.172
  808.2 17.4 %fusion.170 = f32[10,512,2048]{2,1,0:T(8,128)} fusion(bf16[2048,10,32]{0,2,1:T(8,128)(2,1)S(1)} %get-tuple-element.806, bf16[4,512,10,32]{1,3,2,0:T(8,128)(2,1)} %get-tuple-element.802, s32[]{:T(128)S(6)} %copy.58), kind=kOutput, calls=%fused_computation.51.clone.clone.1 | convolution fusion | flops 671088640 | bytes 43581444 | tf_op jit(solution)/shard_map/while/body/eval_jaxpr/qhe,khe->hqk/dot_general | solution.py:44
  825.5 20.7 %select_add_fusion.3 = f32[2048,10,32]{0,2,1:T(8,128)} fusion(f32[2048,10,32]{0,2,1:T(8,128)} %get-tuple-element.784, f32[10,512,2048]{2,1,0:T(8,128)} %fusion.170, f32[10,512]{1,0:T(8,128)S(1)} %dynamic-slice_bitcast_fusion.3, pred[512,2048]{1,0:T(8,128)(4,1)S(1)} %or_and_fusion.7, pred[]{:T(512)S(6)} %compare.36, ...), kind=kOutput, calls=%fused_computation.43.clone.clone.1 | convolution fusion | flops 714342400 | bytes 48582660 | tf_op jit(solution)/shard_map/while/body/eval_jaxpr/hqk,qhe->khe/dot_general | solution.py:107
  846.2 30.2 %multiply_reduce_fusion.6 = (f32[10,512]{1,0:T(8,128)S(1)}, f32[10,512,2048]{2,1,0:T(8,128)}) fusion(f32[10,512,2048]{2,1,0:T(8,128)} %fusion.170, f32[10,512]{1,0:T(8,128)S(1)} %dynamic-slice_bitcast_fusion.3, pred[512,2048]{1,0:T(8,128)(4,1)S(1)} %or_and_fusion.7, bf16[2048,10,32]{0,2,1:T(8,128)(2,1)} %get-tuple-element.809, ...), kind=kOutput, calls=%fused_computation.33.clone.clone.1 | convolution fusion | flops 723512320 | bytes 86614016 | tf_op jit(solution)/shard_map/while/body/eval_jaxpr/qhe,khe->hqk/dot_general | solution.py:91
  876.4 34.2 %multiply_convert_fusion.4 = bf16[10,512,2048]{2,1,0:T(8,128)(2,1)} fusion(f32[10,512,2048]{2,1,0:T(8,128)} %get-tuple-element.728, f32[10,512,2048]{2,1,0:T(8,128)} %fusion.170, f32[10,512]{1,0:T(8,128)S(1)} %get-tuple-element.729, f32[10,512]{1,0:T(8,128)S(1)} %dynamic-slice_bitcast_fusion.3, pred[512,2048]{1,0:T(8,128)(4,1)S(1)} %or_and_fusion.7), kind=kLoop, calls=%fused_computation.32.clone.clone.1 | loop fusion | flops 62914560 | bytes 105947136 | tf_op jit(solution)/shard_map/while/body/eval_jaxpr/convert_element_type | solution.py:95
  910.6 10.7 fusion.172
  935.3 17.4 %fusion.170 = f32[10,512,2048]{2,1,0:T(8,128)} fusion(bf16[2048,10,32]{0,2,1:T(8,128)(2,1)S(1)} %get-tuple-element.806, bf16[4,512,10,32]{1,3,2,0:T(8,128)(2,1)} %get-tuple-element.802, s32[]{:T(128)S(6)} %copy.58), kind=kOutput, calls=%fused_computation.51.clone.clone.1 | convolution fusion | flops 671088640 | bytes 43581444 | tf_op jit(solution)/shard_map/while/body/eval_jaxpr/qhe,khe->hqk/dot_general | solution.py:44
  952.7 20.7 %select_add_fusion.3 = f32[2048,10,32]{0,2,1:T(8,128)} fusion(f32[2048,10,32]{0,2,1:T(8,128)} %get-tuple-element.784, f32[10,512,2048]{2,1,0:T(8,128)} %fusion.170, f32[10,512]{1,0:T(8,128)S(1)} %dynamic-slice_bitcast_fusion.3, pred[512,2048]{1,0:T(8,128)(4,1)S(1)} %or_and_fusion.7, pred[]{:T(512)S(6)} %compare.36, ...), kind=kOutput, calls=%fused_computation.43.clone.clone.1 | convolution fusion | flops 714342400 | bytes 48582660 | tf_op jit(solution)/shard_map/while/body/eval_jaxpr/hqk,qhe->khe/dot_general | solution.py:107
  973.4 30.2 %multiply_reduce_fusion.6 = (f32[10,512]{1,0:T(8,128)S(1)}, f32[10,512,2048]{2,1,0:T(8,128)}) fusion(f32[10,512,2048]{2,1,0:T(8,128)} %fusion.170, f32[10,512]{1,0:T(8,128)S(1)} %dynamic-slice_bitcast_fusion.3, pred[512,2048]{1,0:T(8,128)(4,1)S(1)} %or_and_fusion.7, bf16[2048,10,32]{0,2,1:T(8,128)(2,1)} %get-tuple-element.809, ...), kind=kOutput, calls=%fused_computation.33.clone.clone.1 | convolution fusion | flops 723512320 | bytes 86614016 | tf_op jit(solution)/shard_map/while/body/eval_jaxpr/qhe,khe->hqk/dot_general | solution.py:91
  1003.6 34.2 %multiply_convert_fusion.4 = bf16[10,512,2048]{2,1,0:T(8,128)(2,1)} fusion(f32[10,512,2048]{2,1,0:T(8,128)} %get-tuple-element.728, f32[10,512,2048]{2,1,0:T(8,128)} %fusion.170, f32[10,512]{1,0:T(8,128)S(1)} %get-tuple-element.729, f32[10,512]{1,0:T(8,128)S(1)} %dynamic-slice_bitcast_fusion.3, pred[512,2048]{1,0:T(8,128)(4,1)S(1)} %or_and_fusion.7), kind=kLoop, calls=%fused_computation.32.clone.clone.1 | loop fusion | flops 62914560 | bytes 105947136 | tf_op jit(solution)/shard_map/while/body/eval_jaxpr/convert_element_type | solution.py:95
  1062.4 17.4 %fusion.170 = f32[10,512,2048]{2,1,0:T(8,128)} fusion(bf16[2048,10,32]{0,2,1:T(8,128)(2,1)S(1)} %get-tuple-element.806, bf16[4,512,10,32]{1,3,2,0:T(8,128)(2,1)} %get-tuple-element.802, s32[]{:T(128)S(6)} %copy.58), kind=kOutput, calls=%fused_computation.51.clone.clone.1 | convolution fusion | flops 671088640 | bytes 43581444 | tf_op jit(solution)/shard_map/while/body/eval_jaxpr/qhe,khe->hqk/dot_general | solution.py:44
  1079.8 20.7 %select_add_fusion.3 = f32[2048,10,32]{0,2,1:T(8,128)} fusion(f32[2048,10,32]{0,2,1:T(8,128)} %get-tuple-element.784, f32[10,512,2048]{2,1,0:T(8,128)} %fusion.170, f32[10,512]{1,0:T(8,128)S(1)} %dynamic-slice_bitcast_fusion.3, pred[512,2048]{1,0:T(8,128)(4,1)S(1)} %or_and_fusion.7, pred[]{:T(512)S(6)} %compare.36, ...), kind=kOutput, calls=%fused_computation.43.clone.clone.1 | convolution fusion | flops 714342400 | bytes 48582660 | tf_op jit(solution)/shard_map/while/body/eval_jaxpr/hqk,qhe->khe/dot_general | solution.py:107
  1100.5 30.2 %multiply_reduce_fusion.6 = (f32[10,512]{1,0:T(8,128)S(1)}, f32[10,512,2048]{2,1,0:T(8,128)}) fusion(f32[10,512,2048]{2,1,0:T(8,128)} %fusion.170, f32[10,512]{1,0:T(8,128)S(1)} %dynamic-slice_bitcast_fusion.3, pred[512,2048]{1,0:T(8,128)(4,1)S(1)} %or_and_fusion.7, bf16[2048,10,32]{0,2,1:T(8,128)(2,1)} %get-tuple-element.809, ...), kind=kOutput, calls=%fused_computation.33.clone.clone.1 | convolution fusion | flops 723512320 | bytes 86614016 | tf_op jit(solution)/shard_map/while/body/eval_jaxpr/qhe,khe->hqk/dot_general | solution.py:91
  1130.7 34.2 %multiply_convert_fusion.4 = bf16[10,512,2048]{2,1,0:T(8,128)(2,1)} fusion(f32[10,512,2048]{2,1,0:T(8,128)} %get-tuple-element.728, f32[10,512,2048]{2,1,0:T(8,128)} %fusion.170, f32[10,512]{1,0:T(8,128)S(1)} %get-tuple-element.729, f32[10,512]{1,0:T(8,128)S(1)} %dynamic-slice_bitcast_fusion.3, pred[512,2048]{1,0:T(8,128)(4,1)S(1)} %or_and_fusion.7), kind=kLoop, calls=%fused_computation.32.clone.clone.1 | loop fusion | flops 62914560 | bytes 105947136 | tf_op jit(solution)/shard_map/while/body/eval_jaxpr/convert_element_type | solution.py:95
  1164.9 10.7 fusion.172
  1201.3 12.4 fusion.93
  1213.7 13.1 fusion.94
  1235.4 62.3 %all-reduce.1 = (f32[2,320]{1,0:T(2,128)}, f32[2560]{0:T(1024)}) all-reduce(f32[2,320]{1,0:T(2,128)S(1)} %pad_maximum_fusion.3, f32[2560]{0:T(1024)S(1)} %copy-done.55), channel_id=1, replica_groups=mesh['dp'=16,'tensor'=2] {'dp'}, use_global_device_ids=true, to_apply=%region_26.27 | all-reduce | flops 3200 | bytes 25600 | tf_op jit(solution)/shard_map/psum | solution.py:273
  1305.0 39.1 %all-reduce = (f32[640]{0:T(1024)}, f32[640]{0:T(1024)}, f32[640]{0:T(1024)}, f32[640]{0:T(1024)}, f32[640]{0:T(1024)}, /*index=5*/f32[640]{0:T(1024)}) all-reduce(f32[640]{0:T(1024)S(1)} %get-tuple-element.409, f32[640]{0:T(1024)S(1)} %get-tuple-element.412, ...), channel_id=1, replica_groups=mesh['dp'=16,'tensor'=2] {'dp','tensor'}, use_global_device_ids=true, to_apply=%region_20.21 | all-reduce | flops 3840 | bytes 30720 | tf_op jit(solution)/shard_map/psum | solution.py:261
  1344.1 222.1 %all-reduce.5.cloned.1.call-done = (f32[3,640,320]{1,2,0:T(8,128)}, f32[320,640]{1,0:T(8,128)}, f32[640,2560]{1,0:T(8,128)}, f32[2560,640]{1,0:T(8,128)}) async-done(((f32[3,640,320]{1,2,0:T(8,128)}, f32[320,640]{1,0:T(8,128)}, f32[640,2560]{1,0:T(8,128)}, f32[2560,640]{1,0:T(8,128)}), (f32[3,640,320]{1,2,0:T(8,128)}, f32[320,640]{1,0:T(8,128)}, f32[640,2560]{1,0:T(8,128)}, ...) | async-done | bytes 16384016 | tf_op jit(solution)/shard_map/psum | solution.py:273
  (313 shorter events, 177.2 us)
Async XLA Ops:
  7.2 421.2 %copy-start = (bf16[640,2560]{1,0:T(8,128)(2,1)S(1)}, bf16[640,2560]{1,0:T(8,128)(2,1)}, u32[]{:S(2)}) copy-start(bf16[640,2560]{1,0:T(8,128)(2,1)} %param.33) | copy-start | bytes 9830404
  7.2 48.4 %all-gather.5.cloned.1.call-start = ((), (), s32[]{:S(2)}) async-start(), calls=%async_computation.4 | async-start | bytes 3932160 | tf_op jit(solution)/shard_map/all_gather | solution.py:157
  13.7 369.3 %reduce-scatter.5.cloned.1.call-start = ((), (), s32[]{:S(2)}) async-start(), calls=%async_computation.5 | async-start | bytes 7864320 | tf_op jit(solution)/shard_map/reduce_scatter | solution.py:176
  17.1 43.8 %copy-start.48 = (pred[2,1024]{1,0:T(4,128)(4,1)}, pred[2,1024]{1,0:T(4,128)(4,1)S(1)}, u32[]{:S(2)}) copy-start(pred[2,1024]{1,0:T(4,128)(4,1)S(1)} %not_and_fusion) | copy-start | bytes 6148
  97.0 19.3 %copy-start.9 = (bf16[2048,10,32]{0,2,1:T(8,128)(2,1)S(1)}, bf16[2048,10,32]{0,2,1:T(8,128)(2,1)}, u32[]{:S(2)}) copy-start(bf16[2048,10,32]{0,2,1:T(8,128)(2,1)} %get-tuple-element.762) | copy-start | bytes 3932164 | tf_op jit(solution)/shard_map/while
  97.0 19.3 %copy-start.22 = (bf16[4,512,10,32]{1,3,2,0:T(8,128)(2,1)S(1)}, bf16[4,512,10,32]{1,3,2,0:T(8,128)(2,1)}, u32[]{:S(2)}) copy-start(bf16[4,512,10,32]{1,3,2,0:T(8,128)(2,1)} %get-tuple-element.743) | copy-start | bytes 3932164 | tf_op jit(solution)/shard_map/while
  155.1 19.3 %copy-start.9 = (bf16[2048,10,32]{0,2,1:T(8,128)(2,1)S(1)}, bf16[2048,10,32]{0,2,1:T(8,128)(2,1)}, u32[]{:S(2)}) copy-start(bf16[2048,10,32]{0,2,1:T(8,128)(2,1)} %get-tuple-element.762) | copy-start | bytes 3932164 | tf_op jit(solution)/shard_map/while
  155.1 19.3 %copy-start.22 = (bf16[4,512,10,32]{1,3,2,0:T(8,128)(2,1)S(1)}, bf16[4,512,10,32]{1,3,2,0:T(8,128)(2,1)}, u32[]{:S(2)}) copy-start(bf16[4,512,10,32]{1,3,2,0:T(8,128)(2,1)} %get-tuple-element.743) | copy-start | bytes 3932164 | tf_op jit(solution)/shard_map/while
  213.2 19.3 %copy-start.9 = (bf16[2048,10,32]{0,2,1:T(8,128)(2,1)S(1)}, bf16[2048,10,32]{0,2,1:T(8,128)(2,1)}, u32[]{:S(2)}) copy-start(bf16[2048,10,32]{0,2,1:T(8,128)(2,1)} %get-tuple-element.762) | copy-start | bytes 3932164 | tf_op jit(solution)/shard_map/while
  213.2 19.3 %copy-start.22 = (bf16[4,512,10,32]{1,3,2,0:T(8,128)(2,1)S(1)}, bf16[4,512,10,32]{1,3,2,0:T(8,128)(2,1)}, u32[]{:S(2)}) copy-start(bf16[4,512,10,32]{1,3,2,0:T(8,128)(2,1)} %get-tuple-element.743) | copy-start | bytes 3932164 | tf_op jit(solution)/shard_map/while
  271.3 19.3 %copy-start.9 = (bf16[2048,10,32]{0,2,1:T(8,128)(2,1)S(1)}, bf16[2048,10,32]{0,2,1:T(8,128)(2,1)}, u32[]{:S(2)}) copy-start(bf16[2048,10,32]{0,2,1:T(8,128)(2,1)} %get-tuple-element.762) | copy-start | bytes 3932164 | tf_op jit(solution)/shard_map/while
  271.3 19.3 %copy-start.22 = (bf16[4,512,10,32]{1,3,2,0:T(8,128)(2,1)S(1)}, bf16[4,512,10,32]{1,3,2,0:T(8,128)(2,1)}, u32[]{:S(2)}) copy-start(bf16[4,512,10,32]{1,3,2,0:T(8,128)(2,1)} %get-tuple-element.743) | copy-start | bytes 3932164 | tf_op jit(solution)/shard_map/while
  317.1 66.0 %copy-start.58 = (f32[640]{0:T(1024)S(1)}, f32[640]{0:T(1024)}, u32[]{:S(2)}) copy-start(f32[640]{0:T(1024)} %param.30) | copy-start | bytes 7684
  317.1 111.3 %all-gather.7.cloned.1.call-start = ((), (), s32[]{:S(2)}) async-start(), calls=%async_computation.6 | async-start | bytes 3932160 | tf_op jit(solution)/shard_map/all_gather | solution.py:186
  387.6 40.7 %copy-start.68 = (f32[2560]{0:T(1024)S(1)}, f32[2560]{0:T(1024)}, u32[]{:S(2)}) copy-start(f32[2560]{0:T(1024)} %param.34) | copy-start | bytes 30724
  389.2 93.0 %all-gather.9.cloned.1.call-start = ((), (), s32[]{:S(2)}) async-start(), calls=%async_computation.8 | async-start | bytes 3932160 | tf_op jit(solution)/shard_map/all_gather | solution.py:200
  389.8 197.1 %reduce-scatter.9.cloned.1.call-start = ((), (), s32[]{:S(2)}) async-start(), calls=%async_computation.9 | async-start | bytes 7864320 | tf_op jit(solution)/shard_map/reduce_scatter | solution.py:210
  520.9 105.7 %reduce-scatter.7.cloned.1.call-start = ((), (), s32[]{:S(2)}) async-start(), calls=%async_computation.7 | async-start | bytes 3932160 | tf_op jit(solution)/shard_map/reduce_scatter | solution.py:191
  521.0 65.9 %copy-start.35 = (f32[1024]{0:T(1024)S(1)}, f32[1024]{0:T(1024)}, u32[]{:S(2)}) copy-start(f32[1024]{0:T(1024)} %copy-done.34) | copy-start | bytes 12292
  521.0 65.9 %copy-start.41 = (f32[1024]{0:T(1024)S(1)}, f32[1024]{0:T(1024)}, u32[]{:S(2)}) copy-start(f32[1024]{0:T(1024)} %copy-done.40) | copy-start | bytes 12292
  521.0 65.9 %copy-start.51 = (f32[640]{0:T(1024)S(1)}, f32[640]{0:T(1024)}, u32[]{:S(2)}) copy-start(f32[640]{0:T(1024)} %param.31) | copy-start | bytes 7684
  534.2 52.6 %copy-start.6 = (f32[1024,640]{1,0:T(8,128)S(1)}, f32[1024,640]{1,0:T(8,128)}, u32[]{:S(2)}) copy-start(f32[1024,640]{1,0:T(8,128)} %copy-done.5) | copy-start | bytes 7864324
  534.3 55.9 %copy-start.47 = (f32[1024]{0:T(1024)S(1)}, f32[1024]{0:T(1024)}, u32[]{:S(2)}) copy-start(f32[1024]{0:T(1024)} %copy-done.46) | copy-start | bytes 12292
  534.3 92.4 %copy-start.59 = (f32[640]{0:T(1024)S(1)}, f32[640]{0:T(1024)}, u32[]{:S(2)}) copy-start(f32[640]{0:T(1024)} %param.36) | copy-start | bytes 7684
  534.3 137.5 %all-gather.11.cloned.1.call-start = ((), (), s32[]{:S(2)}) async-start(), calls=%async_computation.10 | async-start | bytes 3932160 | tf_op jit(solution)/shard_map/all_gather | solution.py:220
  630.5 41.3 %copy-start.31 = (bf16[320,640]{1,0:T(8,128)(2,1)S(1)}, bf16[320,640]{1,0:T(8,128)(2,1)}, u32[]{:S(2)}) copy-start(bf16[320,640]{1,0:T(8,128)(2,1)} %param.29) | copy-start | bytes 1228804
  632.7 665.0 %reduce-scatter.11.cloned.1.call-start = ((), (), s32[]{:S(2)}) async-start(), calls=%async_computation.11 | async-start | bytes 7864320 | tf_op jit(solution)/shard_map/reduce_scatter | solution.py:249
  749.3 34.2 %copy-start.15 = (bf16[4,512,10,32]{1,3,2,0:T(8,128)(2,1)S(1)}, bf16[4,512,10,32]{1,3,2,0:T(8,128)(2,1)}, u32[]{:S(2)}) copy-start(bf16[4,512,10,32]{1,3,2,0:T(8,128)(2,1)} %get-tuple-element.785) | copy-start | bytes 3932164 | tf_op jit(solution)/shard_map/while
  783.5 10.7 copy-start.3
  794.2 9.5 copy-start.16
  876.4 34.2 %copy-start.15 = (bf16[4,512,10,32]{1,3,2,0:T(8,128)(2,1)S(1)}, bf16[4,512,10,32]{1,3,2,0:T(8,128)(2,1)}, u32[]{:S(2)}) copy-start(bf16[4,512,10,32]{1,3,2,0:T(8,128)(2,1)} %get-tuple-element.785) | copy-start | bytes 3932164 | tf_op jit(solution)/shard_map/while
  910.6 10.7 copy-start.3
  921.3 9.5 copy-start.16
  1003.6 34.2 %copy-start.15 = (bf16[4,512,10,32]{1,3,2,0:T(8,128)(2,1)S(1)}, bf16[4,512,10,32]{1,3,2,0:T(8,128)(2,1)}, u32[]{:S(2)}) copy-start(bf16[4,512,10,32]{1,3,2,0:T(8,128)(2,1)} %get-tuple-element.785) | copy-start | bytes 3932164 | tf_op jit(solution)/shard_map/while
  1037.8 10.7 copy-start.3
  1048.5 9.5 copy-start.16
  1130.7 34.2 %copy-start.15 = (bf16[4,512,10,32]{1,3,2,0:T(8,128)(2,1)S(1)}, bf16[4,512,10,32]{1,3,2,0:T(8,128)(2,1)}, u32[]{:S(2)}) copy-start(bf16[4,512,10,32]{1,3,2,0:T(8,128)(2,1)} %get-tuple-element.785) | copy-start | bytes 3932164 | tf_op jit(solution)/shard_map/while
  1164.9 10.7 copy-start.3
  1175.6 9.5 copy-start.16
  1201.2 364.9 %all-reduce.5.cloned.1.call-start = ((), (), s32[]{:S(2)}) async-start(), calls=%async_computation.12 | async-start | bytes 32768000 | tf_op jit(solution)/shard_map/psum | solution.py:273
  1201.3 12.4 copy-start.65
  1213.7 13.1 copy-start.20
  1213.7 13.1 copy-start.66
  1234.7 63.0 %copy-start.8 = (bf16[1024,640]{1,0:T(8,128)(2,1)S(1)}, bf16[1024,640]{1,0:T(8,128)(2,1)}, u32[]{:S(2)}) copy-start(bf16[1024,640]{1,0:T(8,128)(2,1)} %param.21) | copy-start | bytes 3932164
  1234.7 63.0 %copy-start.33 = (f32[1024]{0:T(1024)S(1)}, f32[1024]{0:T(1024)}, u32[]{:S(2)}) copy-start(f32[1024]{0:T(1024)} %copy-done.32) | copy-start | bytes 12292
  1234.7 63.0 %copy-start.39 = (f32[640]{0:T(1024)S(1)}, f32[640]{0:T(1024)}, u32[]{:S(2)}) copy-start(f32[640]{0:T(1024)} %param.25) | copy-start | bytes 7684
  1234.7 65.8 %copy-start.45 = (f32[1024]{0:T(1024)S(1)}, f32[1024]{0:T(1024)}, u32[]{:S(2)}) copy-start(f32[1024]{0:T(1024)} %copy-done.44) | copy-start | bytes 12292
  1234.7 65.8 %copy-start.37 = (f32[1024]{0:T(1024)S(1)}, f32[1024]{0:T(1024)}, u32[]{:S(2)}) copy-start(f32[1024]{0:T(1024)} %copy-done.36) | copy-start | bytes 12292
  (53 other events, 146.2 us)
Sparse Core Ops, SparseCore 0:
  13.9 41.7 all-gather.4
  317.2 65.7 reduce-scatter.4
  389.3 38.9 all-gather.6
  429.8 38.9 all-gather.8
  521.1 65.7 reduce-scatter.8
  589.0 37.6 reduce-scatter.6
  632.8 38.9 all-gather.10
  1201.3 65.7 reduce-scatter.10
  1272.9 293.1 all-reduce.4
where the time goes:
time: 1590 us
  matrix products  651 us (41%)
  waiting for transfers between devices  494 us (31%)
  other arithmetic  261 us (16%)
  blocking collectives  101 us (6%)
  local copies, waits for them, and re-layouts  56.3 us (4%)
  between operations  16.6 us (1%)
    psum x1, waiting for transfers between devices, body(): lax.psum((grad_w_qkv, grad_qv_bias, grad_w_out, grad_w_up, grad_up_bias,...  222 us
    dot_general x8, matrix products, block_scores(): jnp.einsum('qhe,khe->hqk', query_part, key_pair, preferred_element_type=j...  144 us
    convert_element_type x4, other arithmetic, one_block(): grad_scores = (probs * (grad_probs - inner_sum)).astype(jnp.bfloat16)  137 us
    dot_general x4, matrix products, one_block(): jnp.einsum('qhe,khe->hqk', grad_part, value_pair, preferred_element_type=...  121 us
    dot_general x4, matrix products, one_block(): jnp.einsum('hqk,qhe->khe', probs.astype(jnp.bfloat16), grad_part, preferr...  82 us
    reduce_sum x4, other arithmetic, one_block(): row_total = jnp.sum(exponent, axis=-1, keepdims=True)  77.3 us
    dot_general x4, matrix products, one_block(): jnp.einsum('hqk,khe->qhe', prob_low, value_pair, preferred_element_type=j...  67.7 us
    reduce_scatter x1, waiting for transfers between devices, body(): lax.psum_scatter(jnp.dot(rows_part, w_out, preferred_element_type=jnp.flo...  65.9 us
  transfers between devices with their start and end apart: 9, of which 7 were waited for; matrix products, arithmetic and copies ran while one was open for 7% of the time, Pallas kernels for 0%

commit v1 on v0

v1 whole, which is shorter than its diff:
```python
import math
import functools
import jax
import jax.numpy as jnp
from jax import lax
from jax.experimental import pallas as pl
from jax.experimental.pallas import tpu as pltpu
from jax.sharding import PartitionSpec as P

HEAD = 32
LOG2E = 1.0 / math.log(2.0)
F32, BF16 = jnp.float32, jnp.bfloat16


def three_terms(x):
    a = x.astype(BF16)
    r = x - a.astype(F32)
    b = r.astype(BF16)
    c = (r - b.astype(F32)).astype(BF16)
    return a, b, c


def scaled_pair(q_t):
    q_s = q_t.astype(F32) * (LOG2E / math.sqrt(HEAD))
    hi = q_s.astype(BF16)
    return hi, (q_s - hi.astype(F32)).astype(BF16)


def rows16(parts, width):
    row = lax.broadcasted_iota(jnp.int32, (16, width), 0)
    out = jnp.zeros((16, width), F32)
    for i, part in enumerate(parts):
        out = jnp.where(row == i, part, out)
    return out.astype(BF16)


def key_rows(k_t, bias):
    keys = k_t.shape[1]
    aux = rows16([bias, -1.0, -1.0, -1.0], keys)
    pad = jnp.zeros((48, keys), BF16)
    return jnp.concatenate([k_t, k_t, aux, pad], axis=0).T


def fwd_kernel(heads, q_block, chunk, q_ref, k_ref, v_ref, bias_ref, o_ref, l_ref, k_aug, s_a, s_b):
    queries, keys = q_ref.shape[1], k_ref.shape[1]
    steps = [(h, b) for h in range(heads) for b in range(queries // q_block)]
    slots = (s_a, s_b)
    ones = rows16([1.0], keys)

    def scores(step):
        h, b = steps[step]
        slot = slots[step % 2]
        rows = slice(h * HEAD, (h + 1) * HEAD)
        if b == 0:
            k_aug[h % 2] = key_rows(k_ref[rows, :], bias_ref[...])
        hi, lo = scaled_pair(q_ref[rows, b * q_block:(b + 1) * q_block])
        q_aug = jnp.concatenate(
            [hi, lo, rows16([1.0], q_block), jnp.zeros((48, q_block), BF16)], axis=0)
        top = None
        for c in range(keys // chunk):
            s = jnp.dot(k_aug[h % 2, c * chunk:(c + 1) * chunk, :], q_aug, preferred_element_type=F32)
            slot[c * chunk:(c + 1) * chunk, :] = s
            m = jnp.max(s, axis=0, keepdims=True)
            top = m if top is None else jnp.maximum(top, m)
        return top

    def mix(step, top):
        h, b = steps[step]
        slot = slots[step % 2]
        rows = slice(h * HEAD, (h + 1) * HEAD)
        cols = slice(b * q_block, (b + 1) * q_block)
        v_aug = jnp.concatenate([v_ref[rows, :], ones], axis=0)
        acc = jnp.zeros((48, q_block), F32)
        for c in range(keys // chunk):
            p = jnp.exp2(slot[c * chunk:(c + 1) * chunk, :] - top).astype(BF16)
            acc = acc + jnp.dot(v_aug[:, c * chunk:(c + 1) * chunk], p, preferred_element_type=F32)
        total = acc[HEAD:HEAD + 1, :]
        o_ref[rows, cols] = (acc[:HEAD] * (1.0 / total)).astype(BF16)
        l_ref[0, h:h + 1, cols] = top + jnp.log2(total)

    top = scores(0)
    for step in range(len(steps)):
        after = scores(step + 1) if step + 1 < len(steps) else None
        mix(step, top)
        top = after


def attention_forward(q_t, k_t, v_t, bias, heads=2, q_block=256, chunk=512):
    width, queries = q_t.shape
    keys = k_t.shape[1]
    all_heads = width // HEAD
    rows = heads * HEAD
    return pl.pallas_call(
        functools.partial(fwd_kernel, heads, q_block, chunk),
        name="attn_fwd",
        grid=(all_heads // heads,),
        out_shape=(jax.ShapeDtypeStruct((width, queries), BF16),
                   jax.ShapeDtypeStruct((all_heads // heads, heads, queries), F32)),
        in_specs=[pl.BlockSpec((rows, queries), lambda i: (i, 0)),
                  pl.BlockSpec((rows, keys), lambda i: (i, 0)),
                  pl.BlockSpec((rows, keys), lambda i: (i, 0)),
                  pl.BlockSpec((1, keys), lambda i: (0, 0))],
        out_specs=(pl.BlockSpec((rows, queries), lambda i: (i, 0)),
                   pl.BlockSpec((1, heads, queries), lambda i: (i, 0, 0))),
        scratch_shapes=[pltpu.VMEM((2, keys, 128), BF16),
                        pltpu.VMEM((keys, q_block), F32),
                        pltpu.VMEM((keys, q_block), F32)],
        compiler_params=pltpu.CompilerParams(vmem_limit_bytes=56 << 20),
        cost_estimate=pl.CostEstimate(
            flops=16 * 2 * HEAD * 2 * all_heads * queries * keys,
            transcendentals=all_heads * queries * keys,
            bytes_accessed=4 * width * keys * 2),
    )(q_t, k_t, v_t, bias)


def bwd_kernel(heads, q_block, chunk, form, q_ref, k_ref, v_ref, bias_ref, o_ref, g_ref, l_ref,
               dq_ref, dk_ref, dv_ref, k_aug, v_aug, dk_acc, dv_acc):
    queries, keys = q_ref.shape[1], k_ref.shape[1]
    scale = 1.0 / math.sqrt(HEAD)
    for h in range(heads):
        rows = slice(h * HEAD, (h + 1) * HEAD)
        k_t = k_ref[rows, :]
        k_aug[...] = key_rows(k_t, bias_ref[...])
        minus = rows16([-1.0, -1.0, -1.0], keys)
        v_aug[...] = jnp.concatenate(
            [v_ref[rows, :], minus, jnp.zeros((80, keys), BF16)], axis=0).T
        for b in range(queries // q_block):
            cols = slice(b * q_block, (b + 1) * q_block)
            q_t = q_ref[rows, cols]
            g_t = g_ref[rows, cols]
            hi, lo = scaled_pair(q_t)
            l3 = three_terms(l_ref[0, h:h + 1, cols])
            q_aug = jnp.concatenate(
                [hi, lo, rows16([1.0] + [t.astype(F32) for t in l3], q_block),
                 jnp.zeros((48, q_block), BF16)], axis=0)
            inner = jnp.sum(g_t.astype(F32) * o_ref[rows, cols].astype(F32), axis=0, keepdims=True)
            g_aug = jnp.concatenate(
                [g_t, rows16([t.astype(F32) for t in three_terms(inner)], q_block),
                 jnp.zeros((80, q_block), BF16)], axis=0)
            if form == "stream":
                q_n, g_n = q_t.T, g_t.T
            dq = jnp.zeros((HEAD, q_block), F32)
            for c in range(keys // chunk):
                span = slice(c * chunk, (c + 1) * chunk)
                p = jnp.exp2(jnp.dot(k_aug[span, :], q_aug, preferred_element_type=F32))
                d = p * jnp.dot(v_aug[span, :], g_aug, preferred_element_type=F32)
                p, d = p.astype(BF16), d.astype(BF16)
                if form == "stream":
                    dv = jnp.dot(p, g_n, preferred_element_type=F32)
                    dk = jnp.dot(d, q_n, preferred_element_type=F32)
                    if b == 0:
                        dv_acc[span, :] = dv
                        dk_acc[span, :] = dk
                    else:
                        dv_acc[span, :] += dv
                        dk_acc[span, :] += dk
                else:
                    nt = (((1,), (1,)), ((), ()))
                    dv = lax.dot_general(g_t, p, nt, preferred_element_type=F32)
                    dk = lax.dot_general(q_t, d, nt, preferred_element_type=F32)
                    if b == 0:
                        dv_acc[:, span] = dv
                        dk_acc[:, span] = dk
                    else:
                        dv_acc[:, span] += dv
                        dk_acc[:, span] += dk
                dq = dq + jnp.dot(k_t[:, span], d, preferred_element_type=F32)
            dq_ref[rows, cols] = (dq * scale).astype(BF16)
        if form == "stream":
            dv_ref[rows, :] = dv_acc[...].T.astype(BF16)
            dk_ref[rows, :] = (dk_acc[...].T * scale).astype(BF16)
        else:
            dv_ref[rows, :] = dv_acc[...].astype(BF16)
            dk_ref[rows, :] = (dk_acc[...] * scale).astype(BF16)


def attention_backward(q_t, k_t, v_t, bias, o_t, g_t, lse, heads=2, q_block=512, chunk=512,
                       form="nt", first=0, count=None):
    width, queries = q_t.shape
    keys = k_t.shape[1]
    rows = heads * HEAD
    count = width // rows if count is None else count
    some = lambda i: (i + first, 0)
    acc = (keys, HEAD) if form == "stream" else (HEAD, keys)
    q_spec = pl.BlockSpec((rows, queries), some)
    k_spec = pl.BlockSpec((rows, keys), some)
    out = lambda i: (i, 0)
    return pl.pallas_call(
        functools.partial(bwd_kernel, heads, q_block, chunk, form),
        name="attn_bwd",
        grid=(count,),
        out_shape=(jax.ShapeDtypeStruct((count * rows, queries), BF16),
                   jax.ShapeDtypeStruct((count * rows, keys), BF16),
                   jax.ShapeDtypeStruct((count * rows, keys), BF16)),
        in_specs=[q_spec, k_spec, k_spec, pl.BlockSpec((1, keys), lambda i: (0, 0)), q_spec, q_spec,
                  pl.BlockSpec((1, heads, queries), lambda i: (i + first, 0, 0))],
        out_specs=(pl.BlockSpec((rows, queries), out), pl.BlockSpec((rows, keys), out),
                   pl.BlockSpec((rows, keys), out)),
        scratch_shapes=[pltpu.VMEM((keys, 128), BF16), pltpu.VMEM((keys, 128), BF16),
                        pltpu.VMEM(acc, F32), pltpu.VMEM(acc, F32)],
        compiler_params=pltpu.CompilerParams(vmem_limit_bytes=56 << 20),
        cost_estimate=pl.CostEstimate(
            flops=16 * 5 * HEAD * 2 * count * heads * queries * keys // 2,
            transcendentals=count * heads * queries * keys,
            bytes_accessed=count * rows * (3 * queries + 4 * keys) * 2),
    )(q_t, k_t, v_t, bias, o_t, g_t, lse)

epsilon = 1e-05
masked_score = -1000000000.0


def layer_norm(inputs, gain_vec, bias_vec):
    center = inputs - jnp.mean(inputs, axis=-1, keepdims=True)
    spread = jnp.mean(center * center, axis=-1, keepdims=True)
    return center * lax.rsqrt(spread + epsilon) * gain_vec + bias_vec


def gelu_exact(inputs):
    return jax.nn.gelu(inputs, approximate=False)


def pair_keys(offsets, item_lengths, key_flags):
    seq_len = key_flags.shape[1]
    column = lax.broadcasted_iota(jnp.int32, (2, seq_len), 1)
    second = lax.broadcasted_iota(jnp.int32, (2, seq_len), 0) == 1
    joined = offsets[1] > offsets[0]
    repeat = second & joined & (offsets[1] + column < offsets[0] + seq_len)
    live_keys = (key_flags == 1) & (column < item_lengths[:, None]) & jnp.logical_not(repeat)
    return live_keys, joined


def einsum32(spec, a, b):
    return jnp.einsum(spec, a, b, preferred_element_type=F32)


def body(
    dp_count,
    tokens,
    window_offsets,
    lengths,
    key_mask,
    ln1_gain,
    ln1_bias,
    w_qkv,
    qv_bias,
    w_out,
    out_bias,
    ln2_gain,
    ln2_bias,
    w_up,
    up_bias,
    w_down,
    down_bias,
    out_grad,
):
    side = lax.axis_index("tensor")
    core = lax.axis_index("dp") % 2
    core_groups = [list(range(c, dp_count, 2)) for c in range(2)]

    def swap_side(x):
        return lax.ppermute(x, "tensor", [(0, 1), (1, 0)])

    def swap_core(x):
        return lax.ppermute(x, "dp", [(i, i ^ 1) for i in range(dp_count)])

    def halves(x, axis):
        size = x.shape[axis] // 2
        return (lax.dynamic_slice_in_dim(x, core * size, size, axis),
                lax.dynamic_slice_in_dim(x, (1 - core) * size, size, axis))

    def ordered(first, second, flag, axis):
        return jnp.where(flag == 0, jnp.concatenate([first, second], axis),
                         jnp.concatenate([second, first], axis))

    def whole(shard, axis):
        near, far = halves(shard, axis)
        other_near = swap_side(near)
        return jnp.concatenate([near, far, other_near, swap_core(other_near)], axis)

    def reduced(grad, axis):
        size = grad.shape[axis] // 4
        near, far, other_near, other_far = (
            lax.slice_in_dim(grad, i * size, (i + 1) * size, axis=axis) for i in range(4))
        got = swap_core(jnp.concatenate([far, other_far], axis).astype(BF16))
        got_own, got_other = jnp.split(got, 2, axis)
        across = swap_side((other_near + got_other.astype(F32)).astype(BF16))
        mine = (near + got_own.astype(F32) + across.astype(F32)).astype(BF16)
        mine = lax.psum(mine, "dp", axis_index_groups=core_groups)
        return ordered(mine, swap_core(mine), core, axis).astype(F32)

    w_qkv_all = whole(w_qkv, 2)
    tokens_other = swap_side(tokens)
    biases = jnp.concatenate([qv_bias.reshape(-1), up_bias])
    biases_other = swap_side(biases)
    local = qv_bias.shape[1]

    def local_order(own, other):
        return jnp.concatenate(halves(own, own.ndim - 1) + halves(other, other.ndim - 1), axis=-1)

    qv_all = local_order(qv_bias, biases_other[:2 * local].reshape(2, local))
    up_bias_all = local_order(up_bias, biases_other[2 * local:])
    w_out_all = whole(w_out, 0)
    w_up_all = whole(w_up, 1)
    w_down_all = whole(w_down, 0)

    live, joined = pair_keys(window_offsets, lengths, key_mask)
    live_own = lax.dynamic_index_in_dim(live, side, 0, keepdims=False)
    live_other = lax.dynamic_index_in_dim(live, 1 - side, 0, keepdims=False) & joined
    bias = jnp.where(jnp.concatenate([live_own, live_other]), 0.0, masked_score)[None].astype(F32)

    tokens_f = tokens.astype(F32)
    normed = layer_norm(tokens_f, ln1_gain, ln1_bias).astype(BF16)
    normed_other = layer_norm(tokens_other.astype(F32), ln1_gain, ln1_bias).astype(BF16)
    normed_both = jnp.concatenate([normed, normed_other], axis=0)
    query = (einsum32("td,de->et", normed, w_qkv_all[0]) + qv_all[0][:, None]).astype(BF16)
    key = einsum32("td,de->et", normed_both, w_qkv_all[1]).astype(BF16)
    value = (einsum32("td,de->et", normed_both, w_qkv_all[2]) + qv_all[1][:, None]).astype(BF16)
    heads_out, log_norm = attention_forward(query, key, value, bias)

    residual_mid = tokens_f + (einsum32("et,ed->td", heads_out, w_out_all) + out_bias)
    normed_mid = layer_norm(residual_mid, ln2_gain, ln2_bias).astype(BF16)
    upper = jnp.dot(normed_mid, w_up_all, preferred_element_type=F32) + up_bias_all
    activated = gelu_exact(upper).astype(BF16)
    branch = jnp.dot(activated, w_down_all, preferred_element_type=F32) + down_bias
    layer_out = (residual_mid + branch).astype(BF16)

    grad_w_down = einsum32("tf,td->fd", activated, out_grad)
    grad_w_down = reduced(grad_w_down, 0)
    grad_act = einsum32("td,fd->tf", out_grad, w_down_all)
    _, gelu_back = jax.vjp(gelu_exact, upper)
    grad_upper = gelu_back(grad_act)[0].astype(BF16)
    grad_w_up = reduced(einsum32("td,tf->df", normed_mid, grad_upper), 1)
    grad_up_bias = jnp.sum(grad_upper, axis=0, dtype=F32)
    grad_normed_mid = einsum32("tf,df->td", grad_upper, w_up_all)
    _, norm2_back = jax.vjp(layer_norm, residual_mid, ln2_gain, ln2_bias)
    grad_mid_part, grad_ln2_gain, grad_ln2_bias = norm2_back(grad_normed_mid)
    grad_mid = out_grad.astype(F32) + grad_mid_part
    grad_mid_low = grad_mid.astype(BF16)
    grad_w_out = reduced(einsum32("et,td->ed", heads_out, grad_mid_low), 0)
    grad_heads = einsum32("td,ed->et", grad_mid_low, w_out_all).astype(BF16)
    grad_query, grad_key, grad_value = attention_backward(
        query, key, value, bias, heads_out, grad_heads, log_norm)

    seq_len = tokens.shape[0]
    grad_normed_kv = (einsum32("et,de->td", grad_key, w_qkv_all[1])
                      + einsum32("et,de->td", grad_value, w_qkv_all[2]))
    from_other = swap_side(grad_normed_kv[seq_len:].astype(BF16))
    grad_w_qkv = reduced(jnp.stack([
        einsum32("td,et->de", normed, grad_query),
        einsum32("td,et->de", normed_both, grad_key),
        einsum32("td,et->de", normed_both, grad_value)]), 2)
    grad_qv_bias = jnp.stack([jnp.sum(grad_query, axis=1, dtype=F32),
                              jnp.sum(grad_value, axis=1, dtype=F32)])
    grad_normed = (grad_normed_kv[:seq_len] + einsum32("et,de->td", grad_query, w_qkv_all[0])
                   + from_other.astype(F32))
    _, norm1_back = jax.vjp(layer_norm, tokens_f, ln1_gain, ln1_bias)
    grad_tok_part, grad_ln1_gain, grad_ln1_bias = norm1_back(grad_normed)
    tokens_grad = (grad_mid + grad_tok_part).astype(BF16)
    grad_out_bias = jnp.sum(grad_mid_low, axis=0, dtype=F32)
    grad_down_bias = jnp.sum(out_grad, axis=0, dtype=F32)

    def global_order(x):
        near, far, other_near, other_far = jnp.split(x, 4, axis=-1)
        return ordered(ordered(near, far, core, -1), ordered(other_near, other_far, core, -1), side, -1)

    smalls = [grad_ln1_gain, grad_ln1_bias, grad_ln2_gain, grad_ln2_bias, grad_out_bias,
              grad_down_bias, global_order(grad_qv_bias).reshape(-1), global_order(grad_up_bias)]
    packed = lax.psum(jnp.concatenate(smalls), ("dp", "tensor"))
    width = ln1_gain.shape[0]
    vectors = [packed[i * width:(i + 1) * width] for i in range(6)]
    at = 6 * width
    qv_sum = packed[at:at + 4 * local].reshape(2, 2 * local)
    up_sum = packed[at + 4 * local:]
    grad_qv_bias = lax.dynamic_slice_in_dim(qv_sum, side * local, local, 1)
    grad_up_bias = lax.dynamic_slice_in_dim(up_sum, side * up_bias.shape[0], up_bias.shape[0], 0)
    return (
        layer_out,
        tokens_grad,
        vectors[0],
        vectors[1],
        grad_w_qkv,
        grad_qv_bias,
        grad_w_out,
        vectors[4],
        vectors[2],
        vectors[3],
        grad_w_up,
        grad_up_bias,
        grad_w_down,
        vectors[5],
    )


def solution(mesh):
    in_specs = (
        P(("dp", "tensor"), None),
        P("dp"),
        P("dp"),
        P("dp", None),
        P(),
        P(),
        P(None, None, "tensor"),
        P(None, "tensor"),
        P("tensor", None),
        P(),
        P(),
        P(),
        P(None, "tensor"),
        P("tensor"),
        P("tensor", None),
        P(),
        P(("dp", "tensor"), None),
    )
    out_specs = (
        P(("dp", "tensor"), None),
        P(("dp", "tensor"), None),
        P(),
        P(),
        P(None, None, "tensor"),
        P(None, "tensor"),
        P("tensor", None),
        P(),
        P(),
        P(),
        P(None, "tensor"),
        P("tensor"),
        P("tensor", None),
        P(),
    )
    bound = functools.partial(body, mesh.shape["dp"])
    return jax.shard_map(bound, mesh=mesh, in_specs=in_specs, out_specs=out_specs, check_vma=False)
```

time: 1590 us -> 756 us (0.48)
  matrix products: 651 us -> 181 us
  waiting for transfers between devices: 494 us -> 245 us
  other arithmetic: 261 us -> 51.4 us
  Pallas kernels: 0 us -> 159 us
  blocking collectives: 101 us -> 39.8 us
  local copies, waits for them, and re-layouts: 56.3 us -> 39.7 us
    dot_general x40 -> x18, matrix products: 651 us -> 181 us  [the longest x16 107 us: einsum32(): return jnp.einsum(spec, a, b, preferred_element_type=F32)]
    pallas_call x0 -> x2, Pallas kernels: none -> 159 us  [the longest x1 103 us: attention_backward(): pl.pallas_call(functools.partial(bwd_kernel, heads, q_block, chunk, form)...]
    reduce_scatter x4 -> x0, waiting for transfers between devices: 155 us -> none  [the longest x1 65.9 us: body(): lax.psum_scatter(jnp.dot(rows_part, w_out, preferred_element_type=jnp.flo...]
    ppermute x0 -> x23, waiting for transfers between devices: none -> 121 us  [the longest x11 120 us: swap_side(): return lax.ppermute(x, 'tensor', [(0, 1), (1, 0)])]
    convert_element_type x9 -> x14, other arithmetic: 148 us -> 30.6 us  [the longest x4 13.3 us: reduced(): return ordered(mine, swap_core(mine), core, axis).astype(F32)]
    all_gather x4 -> x0, waiting for transfers between devices: 116 us -> none  [the longest x1 39.1 us: body(): grad_mid_all = lax.all_gather(grad_mid_low, 'tensor', axis=0, tiled=True)]
    psum x1, waiting for transfers between devices: 222 us -> 124 us  [reduced(): mine = lax.psum(mine, 'dp', axis_index_groups=core_groups)]
    reduce_sum x8 -> x4, other arithmetic: 84.1 us -> 8.51 us  [the longest x1 4.96 us: body(): grad_down_bias = jnp.sum(out_grad, axis=0, dtype=F32)]
  transfers between devices with their start and end apart: 9 -> 24, of which waited for: 7 -> 9; matrix products, arithmetic and copies ran while one was open for 7% -> 24% of each run, Pallas kernels for 0% -> 8%
where the time goes in v1:
time: 756 us; the launch traced here: 748 us
  waiting for transfers between devices  245 us (32%)
  matrix products  181 us (24%)
  Pallas kernels  159 us (21%)
  other arithmetic  51.4 us (7%)
  blocking collectives  39.8 us (5%)
  local copies, waits for them, and re-layouts  39.7 us (5%)
  between operations  17.3 us (2%)
  starting transfers between devices  14.5 us (2%)
    psum x1, waiting for transfers between devices, reduced(): mine = lax.psum(mine, 'dp', axis_index_groups=core_groups)  124 us
    ppermute x11, waiting for transfers between devices, swap_side(): return lax.ppermute(x, 'tensor', [(0, 1), (1, 0)])  120 us
    dot_general x16, matrix products, einsum32(): return jnp.einsum(spec, a, b, preferred_element_type=F32)  107 us
    pallas_call x1, Pallas kernels, attention_backward(): pl.pallas_call(functools.partial(bwd_kernel, heads, q_block, chunk, form)...  103 us
    dot_general x1, matrix products, body(): jnp.dot(normed_mid, w_up_all, preferred_element_type=F32) + up_bias_all  58.8 us
    pallas_call x1, Pallas kernels, attention_forward(): pl.pallas_call(functools.partial(fwd_kernel, heads, q_block, chunk), name...  56.3 us
    psum x1, blocking collectives, body(): packed = lax.psum(jnp.concatenate(smalls), ('dp', 'tensor'))  39.8 us
    unnamed x167, local copies, waits for them, and re-layouts  18.5 us
  transfers between devices with their start and end apart: 24, of which 9 were waited for; matrix products, arithmetic and copies ran while one was open for 24% of the time, Pallas kernels for 8%

profile of v1, /device:TPU:0, one launch (start us, length us, event | category | flops | bytes accessed | tf_op | source)
XLA Modules:
  0.0 748.1 jit_solution(3857330117634363093)
XLA Ops:
  8.8 3.0 collective-permute-start.2
  11.8 1.7 constant_dynamic-slice_fusion.5
  13.5 2.3 constant_dynamic-slice_fusion.12
  15.8 1.9 collective-permute-start
  18.6 4.2 constant_dynamic-slice_fusion.3
  29.7 4.0 constant_dynamic-slice_fusion.1
  35.1 2.5 copy.34
  40.2 22.8 %collective-permute-done.3 = bf16[1024,640]{0,1:T(8,128)(2,1)S(1)} collective-permute-done((bf16[1024,640]{0,1:T(8,128)(2,1)S(1)}, bf16[1024,640]{0,1:T(8,128)(2,1)S(1)}, u32[]{:S(2)}, u32[]{:S(2)}) %collective-permute-start.3) | collective-permute-done | bytes 1310752 | tf_op jit(solution)/shard_map/ppermute | solution.py:261
  64.6 2.3 add_convert_fusion.4.q_ref
  66.9 3.7 convolution_convert_fusion.k_ref
  70.6 3.7 add_convert_fusion.v_ref
  74.3 23.9 %collective-permute-done.6 = bf16[640,1280]{1,0:T(8,128)(2,1)} collective-permute-done((bf16[640,1280]{1,0:T(8,128)(2,1)}, bf16[640,1280]{1,0:T(8,128)(2,1)}, u32[]{:S(2)}, u32[]{:S(2)}) %collective-permute-start.6) | collective-permute-done | bytes 1638432 | tf_op jit(solution)/shard_map/ppermute | solution.py:261
  98.2 56.3 %attn_fwd.1 = (bf16[640,1024]{1,0:T(8,128)(2,1)}, f32[10,2,1024]{2,1,0:T(2,128)}) custom-call(bf16[640,1024]{1,0:T(8,128)(2,1)} %add_convert_fusion.4.q_ref, bf16[640,2048]{1,0:T(8,128)(2,1)} %convolution_convert_fusion.k_ref, bf16[640,2048]{1,0:T(8,128)(2,1)} %add_convert_fusion.v_ref, f32[1,2048]{1,0:T(1,128)} %add_select_fusion.bias_ref), custom_call_target="tpu_custom_call" | custom-call | flops 85899345920 | bytes 10485760 | tf_op jit(solution)/shard_map/attn_fwd/pallas_call | solution.py:93
  154.5 2.8 fusion.84
  159.8 58.8 %multiply_convert_fusion = (bf16[1024,5120]{1,0:T(8,128)(2,1)}, f32[1024,5120]{1,0:T(8,128)}, f32[1024,5120]{1,0:T(8,128)}) fusion(f32[5120]{0:T(1024)S(1)} %pad_maximum_fusion.16, bf16[640,1280]{1,0:T(8,128)(2,1)S(1)} %collective-permute-done.7, bf16[640,1280]{1,0:T(8,128)(2,1)} %collective-permute-done.6, bf16[640,1280]{1,0:T(8,128)(2,1)S(1)} %copy-done.18, ...), kind=kOutput, calls=%fused_computation.12 | convolution fusion | flops 7083130880 | bytes 60313600 | tf_op jit(solution)/shard_map/dot_general | solution.py:322
  218.7 27.5 %convert_reduce_fusion = (f32[5120]{0:T(1024)}, bf16[1024,5120]{1,0:T(8,128)(2,1)}) fusion(f32[1024,5120]{1,0:T(8,128)} %get-tuple-element.55, bf16[1024,640]{1,0:T(8,128)(2,1)S(1)} %copy-done.27, bf16[1280,640]{1,0:T(8,128)(2,1)} %collective-permute-done.9, bf16[1280,640]{1,0:T(8,128)(2,1)} %collective-permute-done.8, ...), kind=kOutput, calls=%fused_computation.11 | convolution fusion | flops 6826224640 | bytes 60334080 | tf_op jit(solution)/shard_map/td,fd->tf/dot_general | solution.py:233
  246.3 15.7 %fusion.87 = (bf16[640,5120]{1,0:T(8,128)(2,1)}, f32[640,5120]{1,0:T(8,128)}) fusion(bf16[1024,5120]{1,0:T(8,128)(2,1)} %get-tuple-element.112, f32[1024,640]{0,1:T(8,128)S(1)} %copy-done.3, f32[640]{0:T(1024)S(1)} %copy-done.66, f32[640]{0:T(1024)S(1)} %copy-done.54, f32[1024]{0:T(1024)S(1)} %copy-done.47, f32[1024]{0:T(1024)S(1)} %copy-done.42), kind=kOutput, calls=%fused_computation.207 | convolution fusion | flops 6717440000 | bytes 32781312 | tf_op jit(solution)/shard_map/td,tf->df/dot_general | solution.py:233
  262.0 15.2 %fusion.85 = (f32[640]{0:T(1024)}, f32[1024,640]{1,0:T(8,128)}) fusion(bf16[1024,5120]{1,0:T(8,128)(2,1)} %get-tuple-element.112, bf16[640,1280]{1,0:T(8,128)(2,1)S(1)} %copy-done.70, bf16[640,1280]{1,0:T(8,128)(2,1)} %collective-permute-done.6, bf16[640,1280]{1,0:T(8,128)(2,1)S(1)} %copy-done.19, bf16[640,1280]{1,0:T(8,128)(2,1)} %get-tuple-element.63), kind=kOutput, calls=%fused_computation.205 | convolution fusion | flops 6737755648 | bytes 19663360 | tf_op jit(solution)/shard_map/tf,df->td/dot_general | solution.py:233
  277.3 3.3 copy.35
  280.6 3.2 multiply_reduce_fusion
  286.4 3.5 convolution_convert_fusion.1.g_ref
  290.0 103.1 %attn_bwd.1 = (bf16[640,1024]{1,0:T(8,128)(2,1)}, bf16[640,2048]{1,0:T(8,128)(2,1)}, bf16[640,2048]{1,0:T(8,128)(2,1)}) custom-call(bf16[640,1024]{1,0:T(8,128)(2,1)} %add_convert_fusion.4.q_ref, bf16[640,2048]{1,0:T(8,128)(2,1)} %convolution_convert_fusion.k_ref, bf16[640,2048]{1,0:T(8,128)(2,1)} %add_convert_fusion.v_ref, ...), custom_call_target="tpu_custom_call" | custom-call | flops 107374182400 | bytes 14417920 | tf_op jit(solution)/shard_map/attn_bwd/pallas_call | solution.py:188
  393.1 4.4 convolution_bitcast_fusion.1
  399.0 14.3 %fusion.88 = (bf16[5120,640]{1,0:T(8,128)(2,1)S(1)}, f32[5120,640]{1,0:T(8,128)}) fusion(bf16[1024,5120]{1,0:T(8,128)(2,1)} %get-tuple-element.54, bf16[1024,640]{1,0:T(8,128)(2,1)S(1)} %copy-done.28), kind=kOutput, calls=%fused_computation.208 | convolution fusion | flops 6714163200 | bytes 31457280 | tf_op jit(solution)/shard_map/tf,td->fd/dot_general | solution.py:233
  415.7 2.2 convolution_bitcast_fusion
  424.9 2.3 fusion.46
  427.6 2.1 collective-permute-start.12
  429.7 2.4 fusion.20
  432.2 2.5 fusion.17
  434.7 2.1 collective-permute-start.21
  436.8 2.4 convolution_add_fusion
  440.6 2.1 fusion.49
  442.6 5.9 collective-permute-done.12
  449.6 34.1 %collective-permute-done.18 = bf16[640,1280]{1,0:T(8,128)(2,1)S(1)} collective-permute-done((bf16[640,1280]{1,0:T(8,128)(2,1)S(1)}, bf16[640,1280]{1,0:T(8,128)(2,1)S(1)}, u32[]{:S(2)}, u32[]{:S(2)}) %collective-permute-start.18) | collective-permute-done | bytes 1638432 | tf_op jit(solution)/shard_map/ppermute | solution.py:261
  483.7 3.9 fusion.22
  487.6 31.2 %collective-permute-done.21 = bf16[1280,640]{1,0:T(8,128)(2,1)S(1)} collective-permute-done((bf16[1280,640]{1,0:T(8,128)(2,1)S(1)}, bf16[1280,640]{1,0:T(8,128)(2,1)S(1)}, u32[]{:S(2)}, u32[]{:S(2)}) %collective-permute-start.21) | collective-permute-done | bytes 1638432 | tf_op jit(solution)/shard_map/ppermute | solution.py:261
  518.8 3.8 fusion.19
  524.3 15.5 %add_convert_fusion.2 = bf16[1024,640]{0,1:T(8,128)(2,1)} fusion(f32[1024,640]{0,1:T(8,128)S(1)} %copy-done.4, bf16[1024,5120]{1,0:T(8,128)(2,1)} %get-tuple-element.54, f32[640]{0:T(1024)S(1)} %copy-done.74, bf16[1280,640]{1,0:T(8,128)(2,1)} %collective-permute-done.9, bf16[1280,640]{1,0:T(8,128)(2,1)} %collective-permute-done.8, ...), kind=kOutput, calls=%fused_computation.84 | convolution fusion | flops 6739066880 | bytes 20974080 | tf_op jit(solution)/shard_map/dot_general | solution.py:324
  539.8 2.5 copy.40
  542.3 2.3 convert_reduce_fusion.1
  546.4 4.2 fusion.71
  553.3 123.7 %all-reduce.3.cloned.1.call-done = (bf16[3,640,160]{1,2,0:T(8,128)(2,1)}, bf16[160,640]{1,0:T(8,128)(2,1)}, bf16[640,1280]{1,0:T(8,128)(2,1)}, bf16[1280,640]{1,0:T(8,128)(2,1)}) async-done(((bf16[3,640,160]{1,2,0:T(8,128)(2,1)}, bf16[160,640]{1,0:T(8,128)(2,1)}, bf16[640,1280]{1,0:T(8,128)(2,1)}, bf16[1280,640]{1,0:T(8,128)(2,1)}), (bf16[3,640,160]{1,2,0:T(8,128)(2,1)}, bf16[160,640]{1,0:T(8,128)(2,1)}, ...) | async-done | bytes 4096016 | tf_op jit(solution)/shard_map/psum | solution.py:288
  677.0 5.0 convert_reduce_fusion.3
  682.6 39.8 %psum.35 = f32[10240]{0:T(1024)S(1)} all-reduce(f32[10240]{0:T(1024)S(1)} %fusion.52), channel_id=1, replica_groups=mesh['dp'=16,'tensor'=2] {'dp','tensor'}, use_global_device_ids=true, to_apply=%region_19.20 | all-reduce | flops 10240 | bytes 81920 | tf_op jit(solution)/shard_map/psum | solution.py:368
  722.5 2.4 copy.41
  728.7 1.7 fusion.43
  730.4 5.6 fusion.24
  736.0 5.0 fusion.23
  (277 shorter events, 42.1 us)
Async XLA Ops:
  7.2 669.8 %all-reduce.3.cloned.1.call-start = ((), (), s32[]{:S(2)}) async-start(), calls=%async_computation | async-start | bytes 8192000 | tf_op jit(solution)/shard_map/psum | solution.py:288
  8.8 28.7 %collective-permute-start.2 = (f32[3200]{0:T(1024)S(1)}, f32[3200]{0:T(1024)S(1)}, u32[]{:S(2)}, u32[]{:S(2)}) collective-permute-start(f32[3200]{0:T(1024)S(1)} %pad_maximum_fusion.17), channel_id=1, source_target_pairs={{0,1},{1,0},{2,3},{3,2},{4,5},{5,4},{6,7},{7,6},{8,9},{9,8},{10,11... | collective-permute-start | bytes 38408 | tf_op jit(solution)/shard_map/ppermute | solution.py:261
  13.5 141.0 %copy-start.35 = (bf16[160,640]{1,0:T(8,128)(2,1)}, bf16[160,640]{1,0:T(8,128)(2,1)S(1)}, u32[]{:S(2)}) copy-start(bf16[160,640]{1,0:T(8,128)(2,1)S(1)} %get-tuple-element.72) | copy-start | bytes 614404
  13.5 24.4 %collective-permute-start.4 = (bf16[160,640]{1,0:T(8,128)(2,1)}, bf16[160,640]{1,0:T(8,128)(2,1)}, u32[]{:S(2)}, u32[]{:S(2)}) collective-permute-start(bf16[160,640]{1,0:T(8,128)(2,1)} %get-tuple-element.73), channel_id=1, source_target_pairs={{0,1},{1,0},{2,3},{3,2},{4,5},{5,4},{6,7},{7,6},{8,9},{9,8},{10,11... | collective-permute-start | bytes 614408 | tf_op jit(solution)/shard_map/ppermute | solution.py:261
  15.8 19.2 %collective-permute-start = (bf16[3,640,160]{1,2,0:T(8,128)(2,1)}, bf16[3,640,160]{1,2,0:T(8,128)(2,1)}, u32[]{:S(2)}, u32[]{:S(2)}) collective-permute-start(bf16[3,640,160]{1,2,0:T(8,128)(2,1)} %get-tuple-element.69), channel_id=1, source_target_pairs={{0,1},{1,0},{2,3},{3,2},{4,5},{5,4},{6,7},{7,6},{8,9},{9,8},{10,11... | collective-permute-start | bytes 1843208 | tf_op jit(solution)/shard_map/ppermute | solution.py:261
  18.4 136.1 %copy-start = (bf16[1024,640]{0,1:T(8,128)(2,1)}, bf16[1024,640]{0,1:T(8,128)(2,1)S(1)}, u32[]{:S(2)}) copy-start(bf16[1024,640]{0,1:T(8,128)(2,1)S(1)} %copy.31) | copy-start | bytes 3932164
  18.4 44.5 %collective-permute-start.3 = (bf16[1024,640]{0,1:T(8,128)(2,1)S(1)}, bf16[1024,640]{0,1:T(8,128)(2,1)S(1)}, u32[]{:S(2)}, u32[]{:S(2)}) collective-permute-start(bf16[1024,640]{0,1:T(8,128)(2,1)S(1)} %copy.31), channel_id=1, source_target_pairs={{0,1},{1,0},{2,3},{3,2},{4,5},{5,4},{6,7},{7,6},{8,9},{9,8},{10,11... | collective-permute-start | bytes 3932168 | tf_op jit(solution)/shard_map/ppermute | solution.py:261
  22.7 75.4 %collective-permute-start.6 = (bf16[640,1280]{1,0:T(8,128)(2,1)}, bf16[640,1280]{1,0:T(8,128)(2,1)}, u32[]{:S(2)}, u32[]{:S(2)}) collective-permute-start(bf16[640,1280]{1,0:T(8,128)(2,1)} %get-tuple-element.63), channel_id=1, source_target_pairs={{0,1},{1,0},{2,3},{3,2},{4,5},{5,4},{6,7},{7,6},{8,9},{9,8},{10,11... | collective-permute-start | bytes 4915208 | tf_op jit(solution)/shard_map/ppermute | solution.py:261
  27.9 35.7 %copy-start.39 = (f32[1024]{0:T(1024)}, f32[1024]{0:T(1024)S(1)}, u32[]{:S(2)}) copy-start(f32[1024]{0:T(1024)S(1)} %broadcast_multiply_fusion.2) | copy-start | bytes 12292
  28.9 34.7 %copy-start.44 = (f32[1024]{0:T(1024)}, f32[1024]{0:T(1024)S(1)}, u32[]{:S(2)}) copy-start(f32[1024]{0:T(1024)S(1)} %fusion.53) | copy-start | bytes 12292
  35.0 3.5 collective-permute-start.1
  37.5 121.3 %collective-permute-start.8 = (bf16[1280,640]{1,0:T(8,128)(2,1)}, bf16[1280,640]{1,0:T(8,128)(2,1)}, u32[]{:S(2)}, u32[]{:S(2)}) collective-permute-start(bf16[1280,640]{1,0:T(8,128)(2,1)} %get-tuple-element.61), channel_id=1, source_target_pairs={{0,1},{1,0},{2,3},{3,2},{4,5},{5,4},{6,7},{7,6},{8,9},{9,8},{10,11... | collective-permute-start | bytes 4915208 | tf_op jit(solution)/shard_map/ppermute | solution.py:261
  37.9 116.6 %collective-permute-start.5 = (bf16[160,640]{1,0:T(8,128)(2,1)}, bf16[160,640]{1,0:T(8,128)(2,1)S(1)}, u32[]{:S(2)}, u32[]{:S(2)}) collective-permute-start(bf16[160,640]{1,0:T(8,128)(2,1)} %collective-permute-done.4), channel_id=1, source_target_pairs={{0,2},{2,0},{4,6},{6,4},{8,10},{10,8},{12,14},{14,12},{16,18},{18,... | collective-permute-start | bytes 614408 | tf_op jit(solution)/shard_map/ppermute | solution.py:264
  38.5 25.1 %copy-start.51 = (f32[640]{0:T(1024)S(1)}, f32[640]{0:T(1024)}, u32[]{:S(2)}) copy-start(f32[640]{0:T(1024)} %param.21) | copy-start | bytes 7684
  38.5 25.1 %copy-start.63 = (f32[640]{0:T(1024)S(1)}, f32[640]{0:T(1024)}, u32[]{:S(2)}) copy-start(f32[640]{0:T(1024)} %param.22) | copy-start | bytes 7684
  40.2 30.4 %copy-start.12 = (bf16[3,640,640]{1,2,0:T(8,128)(2,1)}, bf16[3,640,640]{1,2,0:T(8,128)(2,1)S(1)}, u32[]{:S(2)}) copy-start(bf16[3,640,640]{1,2,0:T(8,128)(2,1)S(1)} %pad_maximum_fusion.6) | copy-start | bytes 7372804
  74.3 80.2 %copy-start.73 = (f32[640]{0:T(1024)S(1)}, f32[640]{0:T(1024)}, u32[]{:S(2)}) copy-start(f32[640]{0:T(1024)} %param.26) | copy-start | bytes 7684
  98.2 61.3 %collective-permute-start.7 = (bf16[640,1280]{1,0:T(8,128)(2,1)}, bf16[640,1280]{1,0:T(8,128)(2,1)S(1)}, u32[]{:S(2)}, u32[]{:S(2)}) collective-permute-start(bf16[640,1280]{1,0:T(8,128)(2,1)} %collective-permute-done.6), channel_id=1, source_target_pairs={{0,2},{2,0},{4,6},{6,4},{8,10},{10,8},{12,14},{14,12},{16,18},{18,... | collective-permute-start | bytes 4915208 | tf_op jit(solution)/shard_map/ppermute | solution.py:264
  158.9 59.7 %collective-permute-start.9 = (bf16[1280,640]{1,0:T(8,128)(2,1)}, bf16[1280,640]{1,0:T(8,128)(2,1)}, u32[]{:S(2)}, u32[]{:S(2)}) collective-permute-start(bf16[1280,640]{1,0:T(8,128)(2,1)} %collective-permute-done.8), channel_id=1, source_target_pairs={{0,2},{2,0},{4,6},{6,4},{8,10},{10,8},{12,14},{14,12},{16,18},{18,... | collective-permute-start | bytes 4915208 | tf_op jit(solution)/shard_map/ppermute | solution.py:264
  159.4 59.2 %copy-start.69 = (bf16[640,1280]{1,0:T(8,128)(2,1)}, bf16[640,1280]{1,0:T(8,128)(2,1)S(1)}, u32[]{:S(2)}) copy-start(bf16[640,1280]{1,0:T(8,128)(2,1)S(1)} %collective-permute-done.7) | copy-start | bytes 4915204
  159.8 58.8 %copy-start.16 = (bf16[1280,640]{1,0:T(8,128)(2,1)S(1)}, bf16[1280,640]{1,0:T(8,128)(2,1)}, u32[]{:S(2)}) copy-start(bf16[1280,640]{1,0:T(8,128)(2,1)} %get-tuple-element.60) | copy-start | bytes 4915204
  159.8 58.8 %copy-start.17 = (bf16[1280,640]{1,0:T(8,128)(2,1)S(1)}, bf16[1280,640]{1,0:T(8,128)(2,1)}, u32[]{:S(2)}) copy-start(bf16[1280,640]{1,0:T(8,128)(2,1)} %get-tuple-element.61) | copy-start | bytes 4915204
  159.8 58.8 %copy-start.27 = (bf16[1024,640]{1,0:T(8,128)(2,1)S(1)}, bf16[1024,640]{1,0:T(8,128)(2,1)}, u32[]{:S(2)}) copy-start(bf16[1024,640]{1,0:T(8,128)(2,1)} %param.33) | copy-start | bytes 3932164
  218.7 27.6 %copy-start.3 = (f32[1024,640]{0,1:T(8,128)S(1)}, f32[1024,640]{0,1:T(8,128)}, u32[]{:S(2)}) copy-start(f32[1024,640]{0,1:T(8,128)} %copy-done.2) | copy-start | bytes 7864324
  218.7 27.6 %copy-start.42 = (f32[1024]{0:T(1024)S(1)}, f32[1024]{0:T(1024)}, u32[]{:S(2)}) copy-start(f32[1024]{0:T(1024)} %copy-done.41) | copy-start | bytes 12292
  218.7 27.6 %copy-start.47 = (f32[1024]{0:T(1024)S(1)}, f32[1024]{0:T(1024)}, u32[]{:S(2)}) copy-start(f32[1024]{0:T(1024)} %copy-done.46) | copy-start | bytes 12292
  218.7 27.6 %copy-start.54 = (f32[640]{0:T(1024)S(1)}, f32[640]{0:T(1024)}, u32[]{:S(2)}) copy-start(f32[640]{0:T(1024)} %param.27) | copy-start | bytes 7684
  218.7 27.5 %copy-start.66 = (f32[640]{0:T(1024)S(1)}, f32[640]{0:T(1024)}, u32[]{:S(2)}) copy-start(f32[640]{0:T(1024)} %param.28) | copy-start | bytes 7684
  246.3 15.7 %copy-start.19 = (bf16[640,1280]{1,0:T(8,128)(2,1)S(1)}, bf16[640,1280]{1,0:T(8,128)(2,1)}, u32[]{:S(2)}) copy-start(bf16[640,1280]{1,0:T(8,128)(2,1)} %get-tuple-element.62) | copy-start | bytes 4915204
  286.4 111.0 %slice-start = ((s8[6553600]{0:T(1024)(128)(4,1)}), s8[4194304]{0:T(1024)(128)(4,1)S(1)}, s32[]{:S(2)}) async-start(s8[6553600]{0:T(1024)(128)(4,1)} %bitcast.60), calls=%async_computation.1 | async-start | bytes 8388608
  290.0 103.1 %copy-start.21 = (bf16[1024,640]{0,1:T(8,128)(2,1)S(1)}, bf16[1024,640]{0,1:T(8,128)(2,1)}, u32[]{:S(2)}) copy-start(bf16[1024,640]{0,1:T(8,128)(2,1)} %copy-done.20) | copy-start | bytes 3932164
  290.0 107.5 %slice-start.1 = ((s8[6553600]{0:T(1024)(128)(4,1)}), s8[2359296]{0:T(1024)(128)(4,1)S(1)}, s32[]{:S(2)}) async-start(s8[6553600]{0:T(1024)(128)(4,1)} %bitcast.60), calls=%async_computation.2 | async-start | bytes 4718592
  398.0 31.7 %collective-permute-start.17 = (bf16[640,2560]{1,0:T(8,128)(2,1)S(1)}, bf16[640,2560]{1,0:T(8,128)(2,1)S(1)}, u32[]{:S(2)}, u32[]{:S(2)}) collective-permute-start(bf16[640,2560]{1,0:T(8,128)(2,1)S(1)} %pad_maximum_fusion.3), channel_id=1, source_target_pairs={{0,2},{2,0},{4,6},{6,4},{8,10},{10,8},{12,14},{14,12},{16,18},{18,... | collective-permute-start | bytes 9830408 | tf_op jit(solution)/shard_map/ppermute | solution.py:264
  413.9 18.3 %collective-permute-start.20 = (bf16[2560,640]{1,0:T(8,128)(2,1)S(1)}, bf16[2560,640]{1,0:T(8,128)(2,1)S(1)}, u32[]{:S(2)}, u32[]{:S(2)}) collective-permute-start(bf16[2560,640]{1,0:T(8,128)(2,1)S(1)} %pad_maximum_fusion.4), channel_id=1, source_target_pairs={{0,2},{2,0},{4,6},{6,4},{8,10},{10,8},{12,14},{14,12},{16,18},{18,... | collective-permute-start | bytes 9830408 | tf_op jit(solution)/shard_map/ppermute | solution.py:264
  420.0 7.5 %collective-permute-start.11 = (bf16[3,640,320]{1,2,0:T(8,128)(2,1)S(1)}, bf16[3,640,320]{1,2,0:T(8,128)(2,1)S(1)}, u32[]{:S(2)}, u32[]{:S(2)}) collective-permute-start(bf16[3,640,320]{1,2,0:T(8,128)(2,1)S(1)} %pad_maximum_fusion.7), channel_id=1, source_target_pairs={{0,2},{2,0},{4,6},{6,4},{8,10},{10,8},{12,14},{14,12},{16,18},{18,... | collective-permute-start | bytes 3686408 | tf_op jit(solution)/shard_map/ppermute | solution.py:264
  422.8 4.5 collective-permute-start.14
  427.4 13.2 %collective-permute-start.15 = (bf16[160,640]{1,0:T(8,128)(2,1)S(1)}, bf16[160,640]{1,0:T(8,128)(2,1)S(1)}, u32[]{:S(2)}, u32[]{:S(2)}) collective-permute-start(bf16[160,640]{1,0:T(8,128)(2,1)S(1)} %fusion.47), channel_id=1, source_target_pairs={{0,1},{1,0},{2,3},{3,2},{4,5},{5,4},{6,7},{7,6},{8,9},{9,8},{10,11... | collective-permute-start | bytes 614408 | tf_op jit(solution)/shard_map/ppermute | solution.py:261
  427.6 21.0 %collective-permute-start.12 = (bf16[3,640,160]{1,2,0:T(8,128)(2,1)S(1)}, bf16[3,640,160]{1,2,0:T(8,128)(2,1)S(1)}, u32[]{:S(2)}, u32[]{:S(2)}) collective-permute-start(bf16[3,640,160]{1,2,0:T(8,128)(2,1)S(1)} %fusion.40), channel_id=1, source_target_pairs={{0,1},{1,0},{2,3},{3,2},{4,5},{5,4},{6,7},{7,6},{8,9},{9,8},{10,11... | collective-permute-start | bytes 1843208 | tf_op jit(solution)/shard_map/ppermute | solution.py:261
  432.1 51.6 %collective-permute-start.18 = (bf16[640,1280]{1,0:T(8,128)(2,1)S(1)}, bf16[640,1280]{1,0:T(8,128)(2,1)S(1)}, u32[]{:S(2)}, u32[]{:S(2)}) collective-permute-start(bf16[640,1280]{1,0:T(8,128)(2,1)S(1)} %fusion.20), channel_id=1, source_target_pairs={{0,1},{1,0},{2,3},{3,2},{4,5},{5,4},{6,7},{7,6},{8,9},{9,8},{10,11... | collective-permute-start | bytes 4915208 | tf_op jit(solution)/shard_map/ppermute | solution.py:261
  434.7 84.1 %collective-permute-start.21 = (bf16[1280,640]{1,0:T(8,128)(2,1)S(1)}, bf16[1280,640]{1,0:T(8,128)(2,1)S(1)}, u32[]{:S(2)}, u32[]{:S(2)}) collective-permute-start(bf16[1280,640]{1,0:T(8,128)(2,1)S(1)} %fusion.17), channel_id=1, source_target_pairs={{0,1},{1,0},{2,3},{3,2},{4,5},{5,4},{6,7},{7,6},{8,9},{9,8},{10,11... | collective-permute-start | bytes 4915208 | tf_op jit(solution)/shard_map/ppermute | solution.py:261
  440.4 105.9 %collective-permute-start.10 = (bf16[1024,640]{0,1:T(8,128)(2,1)}, bf16[1024,640]{0,1:T(8,128)(2,1)}, u32[]{:S(2)}, u32[]{:S(2)}) collective-permute-start(bf16[1024,640]{0,1:T(8,128)(2,1)} %slice.257), channel_id=1, source_target_pairs={{0,1},{1,0},{2,3},{3,2},{4,5},{5,4},{6,7},{7,6},{8,9},{9,8},{10,11... | collective-permute-start | bytes 3932168 | tf_op jit(solution)/shard_map/ppermute | solution.py:261
  550.6 126.3 %copy-start.9 = (bf16[1024,640]{0,1:T(8,128)(2,1)S(1)}, bf16[1024,640]{0,1:T(8,128)(2,1)}, u32[]{:S(2)}) copy-start(bf16[1024,640]{0,1:T(8,128)(2,1)} %copy.34) | copy-start | bytes 3932164
  550.7 126.3 %copy-start.50 = (f32[1024]{0:T(1024)S(1)}, f32[1024]{0:T(1024)}, u32[]{:S(2)}) copy-start(f32[1024]{0:T(1024)} %copy-done.49) | copy-start | bytes 12292
  677.0 53.4 %collective-permute-start.22 = (bf16[1280,640]{1,0:T(8,128)(2,1)}, bf16[1280,640]{1,0:T(8,128)(2,1)}, u32[]{:S(2)}, u32[]{:S(2)}) collective-permute-start(bf16[1280,640]{1,0:T(8,128)(2,1)} %get-tuple-element.49), channel_id=1, source_target_pairs={{0,2},{2,0},{4,6},{6,4},{8,10},{10,8},{12,14},{14,12},{16,18},{18,... | collective-permute-start | bytes 4915208 | tf_op jit(solution)/shard_map/ppermute | solution.py:264
  682.0 44.3 %copy-start.37 = (bf16[160,640]{1,0:T(8,128)(2,1)S(1)}, bf16[160,640]{1,0:T(8,128)(2,1)}, u32[]{:S(2)}) copy-start(bf16[160,640]{1,0:T(8,128)(2,1)} %get-tuple-element.47) | copy-start | bytes 614404
  682.0 54.0 %collective-permute-start.19 = (bf16[640,1280]{1,0:T(8,128)(2,1)}, bf16[640,1280]{1,0:T(8,128)(2,1)S(1)}, u32[]{:S(2)}, u32[]{:S(2)}) collective-permute-start(bf16[640,1280]{1,0:T(8,128)(2,1)} %get-tuple-element.48), channel_id=1, source_target_pairs={{0,2},{2,0},{4,6},{6,4},{8,10},{10,8},{12,14},{14,12},{16,18},{18,... | collective-permute-start | bytes 4915208 | tf_op jit(solution)/shard_map/ppermute | solution.py:264
  682.4 46.2 %collective-permute-start.13 = (bf16[3,640,160]{1,2,0:T(8,128)(2,1)S(1)}, bf16[3,640,160]{1,2,0:T(8,128)(2,1)S(1)}, u32[]{:S(2)}, u32[]{:S(2)}) collective-permute-start(bf16[3,640,160]{1,2,0:T(8,128)(2,1)S(1)} %copy-done.31), channel_id=1, source_target_pairs={{0,2},{2,0},{4,6},{6,4},{8,10},{10,8},{12,14},{14,12},{16,18},{18,... | collective-permute-start | bytes 1843208 | tf_op jit(solution)/shard_map/ppermute | solution.py:264
  726.2 1.5 collective-permute-start.16
  (54 other events, 197.6 us)
Sparse Core Ops, SparseCore 0:
  522.7 154.2 all-reduce.2
